TPU v7x, 32 devices: a whole 2x2x4 slice. The times are simulated.
32 devices in a mesh: dp: 8 (over z, y), rep: 4 (over x, core).
Axes of the slice: x: 2, y: 2, z: 4, core: 2. Of those that a mesh axis runs over, the one named last changes fastest.
Arguments:
- grads: bfloat16 [4, 8, 128, 4096], P('rep', 'dp')
- check_weights: int32 [4, 8, 8, 16], P('rep', 'dp'), may hold values from 1 to 8
Outputs:
- reduced: bfloat16 [128, 4096], P(None, 'dp')
- checksums: bfloat16 [8, 4096], P(None, 'dp')
All inputs are finite; a program needn't handle non-finite values.
Results may differ from a plain program's by a relative error of at most 0.0039.
Values may be sent and summed in bfloat16 or wider, within the bound.
No kernel may reach another device: no remote copies, remote signals or barrier semaphores. Data moves between devices by JAX's collectives and lax.ppermute only.
A program may use at most 64 MiB of HBM per device.

v0:
```python
import jax
import jax.numpy as jnp
from jax import lax
from jax.sharding import PartitionSpec as P


def encode(local_grad, weights):
    wsum = jnp.sum(weights, axis=-1).astype(jnp.float32)
    shaped = local_grad.reshape(weights.shape[0], weights.shape[1], local_grad.shape[-1])
    local = jnp.einsum(
        "kb,kbe->ke", weights.astype(jnp.bfloat16), shaped, preferred_element_type=jnp.float32
    )
    return local / wsum[:, None]


def clip_factor(square, total_rows, width):
    return jnp.minimum(
        1.0, 2.0 * jnp.sqrt(jnp.float32(total_rows * width)) / jnp.sqrt(square + 1e-06)
    )


def body(grads, check_weights):
    local_grad = grads[0, 0]
    local_check = encode(local_grad, check_weights[0, 0])
    terms = local_grad.astype(jnp.float32)
    total_rows = local_grad.shape[0]
    width = local_grad.shape[1]
    owned, owned_check = (
        lax.psum_scatter(terms, "dp", scatter_dimension=1, tiled=True),
        lax.psum_scatter(local_check, "dp", scatter_dimension=1, tiled=True),
    )
    owned, owned_check = lax.psum((owned, owned_check), "rep")
    square = lax.psum(jnp.sum(owned * owned), "dp")
    factor = clip_factor(square, total_rows, width)
    return ((factor * owned).astype(jnp.bfloat16), (factor * owned_check).astype(jnp.bfloat16))


def solution(mesh):
    placed = (P("rep", "dp", None, None), P("rep", "dp", None, None))
    return jax.shard_map(
        body, mesh=mesh, in_specs=placed, out_specs=(P(None, "dp"), P(None, "dp")), check_vma=False
    )
```

profile of v0, /device:TPU:0, one launch (start us, length us, event | category | flops | bytes accessed | tf_op | source)
XLA Modules:
  0.0 223.1 jit_solution(16757861987652702588)
XLA Ops:
  7.2 0.0 copy-start
  7.2 0.0 copy-start.1
  7.2 0.0 reduce-scatter.3.cloned.1.call-start
  7.2 2.9 %bitcast_convert_fusion = f32[128,4096]{1,0:T(8,128)} fusion(bf16[1,1,128,4096]{3,2,1,0:T(8,128)(2,1)} %param.2), kind=kLoop, calls=%fused_computation | loop fusion | flops 524288 | bytes 3145728 | tf_op jit(solution)/shard_map/convert_element_type | solution.py:25
  10.1 0.0 reduce-scatter.3.cloned.1.call-update
  10.1 0.0 all-reduce.2.cloned.1.call-start
  10.2 0.0 copy-done.1
  10.2 0.1 fusion.2
  10.3 0.0 copy-done
  10.3 0.3 fusion
  10.6 72.8 %reduce-scatter.3.cloned.1.call-done = f32[128,512]{1,0:T(8,128)} async-done(((f32[128,4096]{1,0:T(8,128)}), f32[128,512]{1,0:T(8,128)}) %reduce-scatter.3.cloned.1.call-update) | async-done | bytes 262160 | tf_op jit(solution)/shard_map/reduce_scatter | solution.py:29
  83.4 0.0 all-reduce.2.cloned.1.call-update
  83.4 0.0 reduce-scatter.5.cloned.1.call-start
  83.5 0.7 bitcast_divide_fusion
  84.2 0.0 reduce-scatter.5.cloned.1.call-update
  84.2 32.9 %all-reduce.2.cloned.1.call-done = f32[128,512]{1,0:T(8,128)} async-done(((f32[128,512]{1,0:T(8,128)}), f32[128,512]{1,0:T(8,128)}) %all-reduce.2.cloned.1.call-update) | async-done | bytes 262160 | tf_op jit(solution)/shard_map/psum | solution.py:32
  117.1 1.6 multiply_reduce_fusion
  118.7 64.2 %reduce-scatter.5.cloned.1.call-done = f32[8,512]{1,0:T(8,128)} async-done(((f32[8,4096]{1,0:T(8,128)}), f32[8,512]{1,0:T(8,128)}) %reduce-scatter.5.cloned.1.call-update) | async-done | bytes 16400 | tf_op jit(solution)/shard_map/reduce_scatter | solution.py:30
  182.9 10.6 %psum.23 = f32[8,512]{1,0:T(8,128)S(1)} all-reduce(f32[8,512]{1,0:T(8,128)} %reduce-scatter.5.cloned.1.call-done), channel_id=1, replica_groups=mesh['dp'=8,'rep'=4] {'rep'}, use_global_device_ids=true, to_apply=%region_6.0 | all-reduce | flops 4096 | bytes 32768 | tf_op jit(solution)/shard_map/psum | solution.py:32
  193.6 20.0 %psum.22 = f32[]{:T(128)} all-reduce(f32[]{:T(128)} %multiply_reduce_fusion), channel_id=1, replica_groups=mesh['dp'=8,'rep'=4] {'dp'}, use_global_device_ids=true, to_apply=%region_3.0 | all-reduce | flops 1 | bytes 8 | tf_op jit(solution)/shard_map/psum | solution.py:33
  214.3 0.6 multiply_convert_fusion.1
  214.9 1.6 multiply_convert_fusion
  (1 shorter events, 0.0 us)
Async XLA Ops:
  7.2 3.1 %copy-start = (bf16[1,1,128,4096]{3,2,1,0:T(8,128)(2,1)S(1)}, bf16[1,1,128,4096]{3,2,1,0:T(8,128)(2,1)}, u32[]{:S(2)}) copy-start(bf16[1,1,128,4096]{3,2,1,0:T(8,128)(2,1)} %param.2) | copy-start | bytes 3145732
  7.2 3.0 %copy-start.1 = (s32[1,1,8,16]{3,2,1,0:T(8,128)S(1)}, s32[1,1,8,16]{3,2,1,0:T(8,128)}, u32[]{:S(2)}) copy-start(s32[1,1,8,16]{3,2,1,0:T(8,128)} %param.3) | copy-start | bytes 1540
  7.2 76.2 %reduce-scatter.3.cloned.1.call-start = ((), (), s32[]{:S(2)}) async-start(), calls=%async_computation.2 | async-start | bytes 2359296 | tf_op jit(solution)/shard_map/reduce_scatter | solution.py:29
  10.1 107.0 %all-reduce.2.cloned.1.call-start = ((), (), s32[]{:S(2)}) async-start(), calls=%async_computation.3 | async-start | bytes 524288 | tf_op jit(solution)/shard_map/psum | solution.py:32
  83.4 99.5 %reduce-scatter.5.cloned.1.call-start = ((), (), s32[]{:S(2)}) async-start(), calls=%async_computation.4 | async-start | bytes 147456 | tf_op jit(solution)/shard_map/reduce_scatter | solution.py:30
Sparse Core Ops, SparseCore 0:
  11.5 71.8 reduce-scatter.2
  85.7 31.3 all-reduce.1
  121.0 61.9 reduce-scatter.4
where the time goes:
time: 223 us
  waiting for transfers between devices  170 us (76%)
  blocking collectives  30.7 us (14%)
  between operations  14.5 us (7%)
  other arithmetic  7.58 us (3%)
    reduce_scatter x1, waiting for transfers between devices, body(): lax.psum_scatter(terms, 'dp', scatter_dimension=1, tiled=True)  72.8 us
    reduce_scatter x1, waiting for transfers between devices, body(): lax.psum_scatter(local_check, 'dp', scatter_dimension=1, tiled=True)  64.2 us
    psum x1, waiting for transfers between devices, body(): owned, owned_check = lax.psum((owned, owned_check), 'rep')  32.9 us
    psum x1, blocking collectives, body(): square = lax.psum(jnp.sum(owned * owned), 'dp')  20 us
    psum x1, blocking collectives, body(): owned, owned_check = lax.psum((owned, owned_check), 'rep')  10.6 us
  transfers between devices with their start and end apart: 3, of which 3 were waited for; matrix products, arithmetic and copies ran while one was open for 1% of the time, Pallas kernels for 0%

commit v1 on v0

v1 whole, which is shorter than its diff:
```python
import functools

import jax
import jax.numpy as jnp
from jax import lax
from jax.experimental import pallas as pl
from jax.experimental.pallas import tpu as pltpu
from jax.sharding import PartitionSpec as P

LANES = 128
SUBLANES = 8
GRANT = pltpu.CompilerParams(vmem_limit_bytes=8 * 1024 * 1024)


def clip_factor(square, total_rows, width):
    return jnp.minimum(
        1.0, 2.0 * jnp.sqrt(jnp.float32(total_rows * width)) / jnp.sqrt(square + 1e-06)
    )


def pack_kernel(grads_ref, weights_ref, out_ref, sem):
    parts, _, cols = out_ref.shape
    rows = grads_ref.shape[0]
    blocks, block = weights_ref.shape
    copies = [
        pltpu.make_async_copy(
            grads_ref.at[:, pl.ds(part * cols, cols)], out_ref.at[part, pl.ds(0, rows), :], sem
        )
        for part in range(parts)
    ]
    for copy in copies:
        copy.start()
    place = lax.broadcasted_iota(jnp.int32, (block, rows), 1)
    spread = (place % block == lax.broadcasted_iota(jnp.int32, (block, rows), 0)).astype(jnp.bfloat16)
    repeated = jnp.dot(
        weights_ref[...].astype(jnp.bfloat16), spread, preferred_element_type=jnp.float32
    )
    owner = lax.broadcasted_iota(jnp.int32, (blocks, rows), 1) // block
    mine = owner == lax.broadcasted_iota(jnp.int32, (blocks, rows), 0)
    diagonal = jnp.where(mine, repeated, 0.0).astype(jnp.bfloat16)
    for part in range(parts):
        out_ref[part, pl.ds(rows, blocks), :] = diagonal
    for copy in copies:
        copy.wait()


def sum_kernel(rows, recv_ref, total_ref, square_ref):
    parts, held, cols = recv_ref.shape
    blocks = held - rows
    total = jnp.zeros((rows, cols), jnp.float32)
    check = jnp.zeros((4 * blocks, cols), jnp.float32)
    for part in range(parts):
        data = recv_ref[part, pl.ds(0, rows), :]
        total += data.astype(jnp.float32)
        weights = recv_ref[part, pl.ds(rows, blocks), :].astype(jnp.float32)
        share = weights / jnp.sum(weights, axis=1, keepdims=True)
        high = share.astype(jnp.bfloat16).astype(jnp.float32)
        rest = share - high
        middle = rest.astype(jnp.bfloat16).astype(jnp.float32)
        low = rest - middle
        terms = jnp.concatenate([high, middle, low, jnp.zeros_like(low)], axis=0)
        check += jnp.dot(terms.astype(jnp.bfloat16), data, preferred_element_type=jnp.float32)
    total_ref[pl.ds(0, rows), :] = total
    total_ref[pl.ds(rows, blocks), :] = (
        check[:blocks] + check[blocks : 2 * blocks] + check[2 * blocks : 3 * blocks]
    )
    square_ref[...] = jnp.broadcast_to(
        jnp.sum(total * total, axis=0, keepdims=True), square_ref.shape
    )


def scale_kernel(rows, width, squares_ref, *refs):
    *total_refs, reduced_ref, check_ref = refs
    cols = total_refs[0].shape[1]
    factor = clip_factor(jnp.sum(squares_ref[...], keepdims=True), rows, width)
    me = lax.axis_index("rep")
    for step, total_ref in enumerate(total_refs):
        at = pl.ds(pl.multiple_of((me ^ step) * cols, cols), cols)
        scaled = (total_ref[...] * factor).astype(jnp.bfloat16)
        reduced_ref[:, at] = scaled[:rows]
        check_ref[:, at] = scaled[rows:]


def small_body(replicas, parts, grads, check_weights):
    local, weights = grads[0, 0], check_weights[0, 0]
    rows, width = local.shape
    blocks = weights.shape[0]
    cols = width // parts
    vmem = pl.BlockSpec(memory_space=pltpu.VMEM)
    packed = pl.pallas_call(
        pack_kernel,
        out_shape=jax.ShapeDtypeStruct((parts, rows + blocks, cols), jnp.bfloat16),
        in_specs=[pl.BlockSpec(memory_space=pl.ANY), vmem],
        out_specs=vmem,
        scratch_shapes=[pltpu.SemaphoreType.DMA],
        compiler_params=GRANT,
        name="pack",
    )(local, weights)
    received = lax.all_to_all(packed, ("dp", "rep"), 0, 0, tiled=True)
    total, square = pl.pallas_call(
        functools.partial(sum_kernel, rows),
        out_shape=(
            jax.ShapeDtypeStruct((rows + blocks, cols), jnp.float32),
            jax.ShapeDtypeStruct((parts, cols), jnp.float32),
        ),
        in_specs=[vmem],
        out_specs=(vmem, vmem),
        compiler_params=GRANT,
        name="add_up",
    )(received)
    totals = [total]
    for step in range(1, replicas):
        totals.append(lax.ppermute(total, "rep", [(i, i ^ step) for i in range(replicas)]))
    squares = lax.all_to_all(square, ("dp", "rep"), 0, 0, tiled=True)
    return pl.pallas_call(
        functools.partial(scale_kernel, rows, width),
        out_shape=(
            jax.ShapeDtypeStruct((rows, replicas * cols), jnp.bfloat16),
            jax.ShapeDtypeStruct((blocks, replicas * cols), jnp.bfloat16),
        ),
        in_specs=[vmem] * (1 + replicas),
        out_specs=(vmem, vmem),
        compiler_params=GRANT,
        name="scale",
    )(squares, *totals)


def large_body(grads, check_weights):
    local, weights = grads[0, 0], check_weights[0, 0]
    rows, width = local.shape
    blocks, block = weights.shape
    wsum = jnp.sum(weights, axis=-1).astype(jnp.float32)
    local_check = jnp.einsum(
        "kb,kbe->ke",
        weights.astype(jnp.bfloat16),
        local.reshape(blocks, block, width),
        preferred_element_type=jnp.float32,
    )
    terms = jnp.concatenate([local.astype(jnp.float32), local_check / wsum[:, None]], axis=0)
    owned = lax.psum(lax.psum_scatter(terms, "dp", scatter_dimension=1, tiled=True), "rep")
    square = lax.psum(jnp.sum(owned[:rows] * owned[:rows]), "dp")
    scaled = (clip_factor(square, rows, width) * owned).astype(jnp.bfloat16)
    return scaled[:rows], scaled[rows:]


def solution(mesh):
    replicas = mesh.shape["rep"]
    parts = replicas * mesh.shape["dp"]
    placed = P("rep", "dp", None, None)

    def step(grads, check_weights):
        rows, width = grads.shape[2:]
        blocks = check_weights.shape[2]
        tiled = (
            width == parts * LANES
            and rows == LANES
            and blocks == SUBLANES
            and replicas & (replicas - 1) == 0
        )
        body = functools.partial(small_body, replicas, parts) if tiled else large_body
        return jax.shard_map(
            body,
            mesh=mesh,
            in_specs=(placed, placed),
            out_specs=(P(None, "dp"), P(None, "dp")),
            check_vma=False,
        )(grads, check_weights)

    return step
```

time: 223 us -> 51.8 us (0.23)
  waiting for transfers between devices: 170 us -> 0.01 us
  blocking collectives: 30.7 us -> 45.3 us
  between operations: 14.5 us -> 0.66 us
  other arithmetic: 7.58 us -> 0 us
    reduce_scatter x2 -> x0, waiting for transfers between devices: 137 us -> none  [the longest x1 72.8 us: body(): lax.psum_scatter(terms, 'dp', scatter_dimension=1, tiled=True)]
    all_to_all x0 -> x2, blocking collectives: none -> 45.3 us  [the longest x1 36.5 us: small_body(): received = lax.all_to_all(packed, ('dp', 'rep'), 0, 0, tiled=True)]
    psum x1 -> x0, waiting for transfers between devices: 32.9 us -> none  [body(): owned, owned_check = lax.psum((owned, owned_check), 'rep')]
    psum x2 -> x0, blocking collectives: 30.7 us -> none  [the longest x1 20 us: body(): square = lax.psum(jnp.sum(owned * owned), 'dp')]
    convert_element_type x4 -> x0, other arithmetic: 5.1 us -> none  [the longest x1 2.87 us: body(): terms = local_grad.astype(jnp.float32)]
  transfers between devices with their start and end apart: 3 -> 3, of which waited for: 3 -> 0; matrix products, arithmetic and copies ran while one was open for 1% -> 0% of each run, Pallas kernels for 0% -> 0%
where the time goes in v1:
time: 51.8 us; the launch traced here: 51.5 us
  blocking collectives  45.3 us (87%)
  starting transfers between devices  1.93 us (4%)
  local copies, waits for them, and re-layouts  1.9 us (4%)
  Pallas kernels  1.7 us (3%)
  between operations  0.66 us (1%)
    all_to_all x1, blocking collectives, small_body(): received = lax.all_to_all(packed, ('dp', 'rep'), 0, 0, tiled=True)  36.5 us
    all_to_all x1, blocking collectives, small_body(): squares = lax.all_to_all(square, ('dp', 'rep'), 0, 0, tiled=True)  8.87 us
    ppermute x3, starting transfers between devices, small_body(): lax.ppermute(total, 'rep', [(i, i ^ step) for i in range(replicas)])  1.93 us
    unnamed x4, local copies, waits for them, and re-layouts  1.9 us
  transfers between devices with their start and end apart: 3, of which 0 were waited for; matrix products, arithmetic and copies ran while one was open for 0% of the time, Pallas kernels for 0%

profile of v1, /device:TPU:0, one launch (start us, length us, event | category | flops | bytes accessed | tf_op | source)
XLA Modules:
  0.0 51.5 jit_solution(2186744276102029291)
XLA Ops:
  0.6 0.0 copy-start
  0.6 1.2 %copy-done = bf16[1,1,128,4096]{3,2,1,0:T(8,128)(2,1)S(1)} copy-done((bf16[1,1,128,4096]{3,2,1,0:T(8,128)(2,1)S(1)}, bf16[1,1,128,4096]{3,2,1,0:T(8,128)(2,1)}, u32[]{:S(2)}) %copy-start) | copy-done | bytes 1048600
  1.9 0.0 copy-start.1
  1.9 0.7 %copy-done.1 = s32[1,1,8,16]{3,2,1,0:T(8,128)S(1)} copy-done((s32[1,1,8,16]{3,2,1,0:T(8,128)S(1)}, s32[1,1,8,16]{3,2,1,0:T(8,128)}, u32[]{:S(2)}) %copy-start.1) | copy-done | bytes 536
  2.5 0.4 pack.1
  3.0 36.5 %all_to_all.16.recv_ref = bf16[32,136,128]{2,1,0:T(8,128)(2,1)S(1)} all-to-all(bf16[32,136,128]{2,1,0:T(8,128)(2,1)S(1)} %pack.1), channel_id=1, replica_groups=mesh['dp'=8,'rep'=4] {'dp','rep'}, dimensions={0} | all-to-all | bytes 2228224 | tf_op jit(solution)/shard_map/all_to_all | solution.py:99
  39.4 0.5 add_up.1
  39.9 0.3 collective-permute-start.2
  40.2 1.0 %collective-permute-start.1 = (f32[136,128]{1,0:T(8,128)S(1)}, f32[136,128]{1,0:T(8,128)S(1)}, u32[]{:S(2)}, u32[]{:S(2)}) collective-permute-start(f32[136,128]{1,0:T(8,128)S(1)} %get-tuple-element.5.refs_0_), channel_id=1, source_target_pairs={{0,2},{1,3},{2,0},{3,1},{4,6},{5,7},{6,4},{7,5},{8,10},{9,11},{10,... | collective-permute-start | bytes 208904 | tf_op jit(solution)/shard_map/ppermute | solution.py:113
  41.2 0.6 %collective-permute-start = (f32[136,128]{1,0:T(8,128)S(1)}, f32[136,128]{1,0:T(8,128)S(1)}, u32[]{:S(2)}, u32[]{:S(2)}) collective-permute-start(f32[136,128]{1,0:T(8,128)S(1)} %get-tuple-element.5.refs_0_), channel_id=1, source_target_pairs={{0,1},{1,0},{2,3},{3,2},{4,5},{5,4},{6,7},{7,6},{8,9},{9,8},{10,11... | collective-permute-start | bytes 208904 | tf_op jit(solution)/shard_map/ppermute | solution.py:113
  41.8 8.9 %all_to_all.17 = f32[32,1,128]{2,1,0:T(1,128)S(1)} all-to-all(f32[32,1,128]{2,1,0:T(1,128)S(1)} %bitcast.8), channel_id=1, replica_groups=mesh['dp'=8,'rep'=4] {'dp','rep'}, dimensions={0} | all-to-all | bytes 32768 | tf_op jit(solution)/shard_map/all_to_all | solution.py:114
  50.7 0.0 collective-permute-done.2.refs_3_
  50.7 0.0 collective-permute-done.1.refs_2_
  50.7 0.0 collective-permute-done.refs_1_
  50.7 0.8 %scale.1 = (bf16[128,512]{1,0:T(8,128)(2,1)}, bf16[8,512]{1,0:T(8,128)(2,1)}) custom-call(f32[32,128]{1,0:T(8,128)S(1)} %bitcast.7, f32[136,128]{1,0:T(8,128)S(1)} %get-tuple-element.5.refs_0_, f32[136,128]{1,0:T(8,128)S(1)} %collective-permute-done.refs_1_, f32[136,128]{1,0:T(8,128)S(1)} %collective-permute-done.1.refs_2_, ...), custom_call_target="tpu_custom_call" | custom-call | tf_op jit(solution)/shard_map/scale/pallas_call | solution.py:115
Async XLA Ops:
  0.6 1.2 %copy-start = (bf16[1,1,128,4096]{3,2,1,0:T(8,128)(2,1)S(1)}, bf16[1,1,128,4096]{3,2,1,0:T(8,128)(2,1)}, u32[]{:S(2)}) copy-start(bf16[1,1,128,4096]{3,2,1,0:T(8,128)(2,1)} %param.2) | copy-start | bytes 3145732
  1.9 0.7 %copy-start.1 = (s32[1,1,8,16]{3,2,1,0:T(8,128)S(1)}, s32[1,1,8,16]{3,2,1,0:T(8,128)}, u32[]{:S(2)}) copy-start(s32[1,1,8,16]{3,2,1,0:T(8,128)} %param.3) | copy-start | bytes 1540
  39.9 10.8 %collective-permute-start.2 = (f32[136,128]{1,0:T(8,128)S(1)}, f32[136,128]{1,0:T(8,128)S(1)}, u32[]{:S(2)}, u32[]{:S(2)}) collective-permute-start(f32[136,128]{1,0:T(8,128)S(1)} %get-tuple-element.5.refs_0_), channel_id=1, source_target_pairs={{0,3},{1,2},{2,1},{3,0},{4,7},{5,6},{6,5},{7,4},{8,11},{9,10},{10,... | collective-permute-start | bytes 208904 | tf_op jit(solution)/shard_map/ppermute | solution.py:113
  40.2 10.5 %collective-permute-start.1 = (f32[136,128]{1,0:T(8,128)S(1)}, f32[136,128]{1,0:T(8,128)S(1)}, u32[]{:S(2)}, u32[]{:S(2)}) collective-permute-start(f32[136,128]{1,0:T(8,128)S(1)} %get-tuple-element.5.refs_0_), channel_id=1, source_target_pairs={{0,2},{1,3},{2,0},{3,1},{4,6},{5,7},{6,4},{7,5},{8,10},{9,11},{10,... | collective-permute-start | bytes 208904 | tf_op jit(solution)/shard_map/ppermute | solution.py:113
  41.2 9.5 %collective-permute-start = (f32[136,128]{1,0:T(8,128)S(1)}, f32[136,128]{1,0:T(8,128)S(1)}, u32[]{:S(2)}, u32[]{:S(2)}) collective-permute-start(f32[136,128]{1,0:T(8,128)S(1)} %get-tuple-element.5.refs_0_), channel_id=1, source_target_pairs={{0,1},{1,0},{2,3},{3,2},{4,5},{5,4},{6,7},{7,6},{8,9},{9,8},{10,11... | collective-permute-start | bytes 208904 | tf_op jit(solution)/shard_map/ppermute | solution.py:113

commit v2 on v1

v2 whole, which is shorter than its diff:
```python
import functools

import jax
import jax.numpy as jnp
from jax import lax
from jax.experimental import pallas as pl
from jax.experimental.pallas import tpu as pltpu
from jax.sharding import Mesh
from jax.sharding import PartitionSpec as P

LANES = 128
SUBLANES = 8
GRANT = pltpu.CompilerParams(vmem_limit_bytes=8 * 1024 * 1024)


def clip_factor(square, total_rows, width):
    return jnp.minimum(
        1.0, 2.0 * jnp.sqrt(jnp.float32(total_rows * width)) / jnp.sqrt(square + 1e-06)
    )


def pack_kernel(grads_hbm, weights_hbm, out_ref, weights_ref, grads_sem, weights_sem):
    parts, held, cols = out_ref.shape
    rows, width = grads_hbm.shape
    blocks, block = weights_ref.shape
    halves = width // (parts * cols)
    fetch = pltpu.make_async_copy(weights_hbm, weights_ref, weights_sem)
    fetch.start()
    copies = [
        pltpu.make_async_copy(
            grads_hbm.at[:, pl.ds((half * parts + part) * cols, cols)],
            out_ref.at[part, pl.ds(half * rows, rows), :],
            grads_sem,
        )
        for half in range(halves)
        for part in range(parts)
    ]
    for copy in copies:
        copy.start()
    fetch.wait()
    place = lax.broadcasted_iota(jnp.int32, (block, rows), 1)
    spread = (place % block == lax.broadcasted_iota(jnp.int32, (block, rows), 0)).astype(jnp.bfloat16)
    repeated = jnp.dot(
        weights_ref[...].astype(jnp.bfloat16), spread, preferred_element_type=jnp.float32
    )
    owner = lax.broadcasted_iota(jnp.int32, (blocks, rows), 1) // block
    mine = owner == lax.broadcasted_iota(jnp.int32, (blocks, rows), 0)
    diagonal = jnp.where(mine, repeated, 0.0).astype(jnp.bfloat16)
    for part in range(parts):
        out_ref[part, pl.ds(held - blocks, blocks), :] = diagonal
    for copy in copies:
        copy.wait()


def sum_kernel(rows, recv_ref, mine_ref, other_ref):
    parts, held, cols = recv_ref.shape
    blocks = mine_ref.shape[0] - rows
    me = lax.axis_index("far")
    places = (me, 1 - me)
    totals = [jnp.zeros((rows, cols), jnp.float32)] * 2
    checks = [jnp.zeros((4 * blocks, cols), jnp.float32)] * 2
    for part in range(parts):
        weights = recv_ref[part, pl.ds(held - blocks, blocks), :].astype(jnp.float32)
        share = weights / jnp.sum(weights, axis=1, keepdims=True)
        high = share.astype(jnp.bfloat16).astype(jnp.float32)
        rest = share - high
        middle = rest.astype(jnp.bfloat16).astype(jnp.float32)
        low = rest - middle
        terms = jnp.concatenate([high, middle, low, jnp.zeros_like(low)], axis=0)
        terms = terms.astype(jnp.bfloat16)
        for i, place in enumerate(places):
            data = recv_ref[part, pl.ds(pl.multiple_of(place * rows, rows), rows), :]
            totals[i] += data.astype(jnp.float32)
            checks[i] += jnp.dot(terms, data, preferred_element_type=jnp.float32)
    for ref, total, check in zip((mine_ref, other_ref), totals, checks, strict=True):
        ref[pl.ds(0, rows), :] = total
        ref[pl.ds(rows, blocks), :] = (
            check[:blocks] + check[blocks : 2 * blocks] + check[2 * blocks : 3 * blocks]
        )


def join_kernel(rows, mine_ref, came_ref, total_ref, square_ref):
    total = mine_ref[...] + came_ref[...]
    total_ref[...] = total
    square_ref[...] = jnp.broadcast_to(
        jnp.sum(total[:rows] * total[:rows], axis=0, keepdims=True), square_ref.shape
    )


def scale_kernel(rows, width, squares_ref, *refs):
    *total_refs, reduced_ref, check_ref = refs
    cols = total_refs[0].shape[1]
    factor = clip_factor(jnp.sum(squares_ref[...], keepdims=True), rows, width)
    me = lax.axis_index("rep")
    for step, total_ref in enumerate(total_refs):
        at = pl.ds(pl.multiple_of((me ^ step) * cols, cols), cols)
        scaled = (total_ref[...] * factor).astype(jnp.bfloat16)
        reduced_ref[:, at] = scaled[:rows]
        check_ref[:, at] = scaled[rows:]


def small_body(sizes, grads, check_weights):
    far, near, replicas = sizes
    local, weights = grads[0, 0], check_weights[0, 0]
    rows, width = local.shape
    blocks = weights.shape[0]
    parts = near * replicas
    cols = width // (far * parts)
    vmem = pl.BlockSpec(memory_space=pltpu.VMEM)
    hbm = pl.BlockSpec(memory_space=pltpu.HBM)
    sums = jax.ShapeDtypeStruct((rows + blocks, cols), jnp.float32)
    packed = pl.pallas_call(
        pack_kernel,
        out_shape=jax.ShapeDtypeStruct((parts, far * rows + blocks, cols), jnp.bfloat16),
        in_specs=[hbm, hbm],
        out_specs=vmem,
        scratch_shapes=[
            pltpu.VMEM(weights.shape, weights.dtype),
            pltpu.SemaphoreType.DMA,
            pltpu.SemaphoreType.DMA,
        ],
        compiler_params=GRANT,
        name="pack",
    )(local, weights)
    received = lax.all_to_all(packed, ("near", "rep"), 0, 0, tiled=True)
    mine, other = pl.pallas_call(
        functools.partial(sum_kernel, rows),
        out_shape=(sums, sums),
        in_specs=[vmem],
        out_specs=(vmem, vmem),
        compiler_params=GRANT,
        name="add_up",
    )(received)
    came = lax.ppermute(other, "far", [(0, 1), (1, 0)])
    total, square = pl.pallas_call(
        functools.partial(join_kernel, rows),
        out_shape=(sums, jax.ShapeDtypeStruct((far * parts, cols), jnp.float32)),
        in_specs=[vmem, vmem],
        out_specs=(vmem, vmem),
        compiler_params=GRANT,
        name="join",
    )(mine, came)
    totals = [total]
    for step in range(1, replicas):
        totals.append(lax.ppermute(total, "rep", [(i, i ^ step) for i in range(replicas)]))
    squares = lax.all_to_all(square, ("far", "near", "rep"), 0, 0, tiled=True)
    return pl.pallas_call(
        functools.partial(scale_kernel, rows, width),
        out_shape=(
            jax.ShapeDtypeStruct((rows, replicas * cols), jnp.bfloat16),
            jax.ShapeDtypeStruct((blocks, replicas * cols), jnp.bfloat16),
        ),
        in_specs=[vmem] * (1 + replicas),
        out_specs=(vmem, vmem),
        compiler_params=GRANT,
        name="scale",
    )(squares, *totals)


def large_body(grads, check_weights):
    local, weights = grads[0, 0], check_weights[0, 0]
    rows, width = local.shape
    blocks, block = weights.shape
    wsum = jnp.sum(weights, axis=-1).astype(jnp.float32)
    local_check = jnp.einsum(
        "kb,kbe->ke",
        weights.astype(jnp.bfloat16),
        local.reshape(blocks, block, width),
        preferred_element_type=jnp.float32,
    )
    terms = jnp.concatenate([local.astype(jnp.float32), local_check / wsum[:, None]], axis=0)
    owned = lax.psum(lax.psum_scatter(terms, "dp", scatter_dimension=1, tiled=True), "rep")
    square = lax.psum(jnp.sum(owned[:rows] * owned[:rows]), "dp")
    scaled = (clip_factor(square, rows, width) * owned).astype(jnp.bfloat16)
    return scaled[:rows], scaled[rows:]


def solution(mesh):
    replicas, columns = mesh.shape["rep"], mesh.shape["dp"]
    far, near = 2, columns // 2

    def step(grads, check_weights):
        rows, width = grads.shape[2:]
        blocks = check_weights.shape[2]
        tiled = (
            width == columns * replicas * LANES
            and rows == LANES
            and blocks == SUBLANES
            and columns % far == 0
            and replicas & (replicas - 1) == 0
        )
        if tiled:
            body = functools.partial(small_body, (far, near, replicas))
            used = Mesh(mesh.devices.reshape(far, near, replicas), ("far", "near", "rep"))
            dp = ("far", "near")
        else:
            body, used, dp = large_body, mesh, "dp"
        placed = P("rep", dp, None, None)
        return jax.shard_map(
            body,
            mesh=used,
            in_specs=(placed, placed),
            out_specs=(P(None, dp), P(None, dp)),
            check_vma=False,
        )(grads, check_weights)

    return step
```

time: 51.8 us -> 45.8 us (0.88)
  blocking collectives: 45.3 us -> 32.8 us
  waiting for transfers between devices: 0.01 us -> 3.83 us
  starting transfers between devices: 1.93 us -> 4.58 us
    all_to_all x2, blocking collectives: 45.3 us -> 32.8 us  [the longest x1 22.6 us: small_body(): received = lax.all_to_all(packed, ('near', 'rep'), 0, 0, tiled=True)]
    ppermute x0 -> x1, waiting for transfers between devices: none -> 3.83 us  [small_body(): came = lax.ppermute(other, 'far', [(0, 1), (1, 0)])]
    ppermute x0 -> x1, starting transfers between devices: none -> 2.65 us  [small_body(): came = lax.ppermute(other, 'far', [(0, 1), (1, 0)])]
  transfers between devices with their start and end apart: 3 -> 4, of which waited for: 0 -> 1; matrix products, arithmetic and copies ran while one was open for 0% -> 0% of each run, Pallas kernels for 0% -> 0%
where the time goes in v2:
time: 45.8 us; the launch traced here: 45.5 us
  blocking collectives  32.8 us (72%)
  starting transfers between devices  4.58 us (10%)
  waiting for transfers between devices  3.83 us (8%)
  local copies, waits for them, and re-layouts  1.9 us (4%)
  Pallas kernels  1.73 us (4%)
  between operations  0.66 us (1%)
    all_to_all x1, blocking collectives, small_body(): received = lax.all_to_all(packed, ('near', 'rep'), 0, 0, tiled=True)  22.6 us
    all_to_all x1, blocking collectives, small_body(): squares = lax.all_to_all(square, ('far', 'near', 'rep'), 0, 0, tiled=True)  10.2 us
    ppermute x1, waiting for transfers between devices, small_body(): came = lax.ppermute(other, 'far', [(0, 1), (1, 0)])  3.83 us
    ppermute x1, starting transfers between devices, small_body(): came = lax.ppermute(other, 'far', [(0, 1), (1, 0)])  2.65 us
    ppermute x3, starting transfers between devices, small_body(): lax.ppermute(total, 'rep', [(i, i ^ step) for i in range(replicas)])  1.92 us
    unnamed x4, local copies, waits for them, and re-layouts  1.9 us
  transfers between devices with their start and end apart: 4, of which 1 were waited for; matrix products, arithmetic and copies ran while one was open for 0% of the time, Pallas kernels for 0%

profile of v2, /device:TPU:0, one launch (start us, length us, event | category | flops | bytes accessed | tf_op | source)
XLA Modules:
  0.0 45.5 jit_solution(17696116822632895283)
XLA Ops:
  0.6 0.0 copy-start
  0.6 1.2 %copy-done = bf16[1,1,128,4096]{3,2,1,0:T(8,128)(2,1)S(1)} copy-done((bf16[1,1,128,4096]{3,2,1,0:T(8,128)(2,1)S(1)}, bf16[1,1,128,4096]{3,2,1,0:T(8,128)(2,1)}, u32[]{:S(2)}) %copy-start) | copy-done | bytes 1048600
  1.9 0.0 copy-start.1
  1.9 0.7 %copy-done.1 = s32[1,1,8,16]{3,2,1,0:T(8,128)S(1)} copy-done((s32[1,1,8,16]{3,2,1,0:T(8,128)S(1)}, s32[1,1,8,16]{3,2,1,0:T(8,128)}, u32[]{:S(2)}) %copy-start.1) | copy-done | bytes 536
  2.5 0.4 pack.1
  3.0 22.6 %all_to_all.16.recv_ref = bf16[16,264,128]{2,1,0:T(8,128)(2,1)S(1)} all-to-all(bf16[16,264,128]{2,1,0:T(8,128)(2,1)S(1)} %pack.1), channel_id=1, replica_groups=mesh['far'=2,'near'=4,'rep'=4] {'near','rep'}, dimensions={0} | all-to-all | bytes 2162688 | tf_op jit(solution)/shard_map/all_to_all | solution.py:125
  25.6 0.5 add_up.1
  26.0 2.7 %collective-permute-start = (f32[136,128]{1,0:T(8,128)S(1)}, f32[136,128]{1,0:T(8,128)S(1)}, u32[]{:S(2)}, u32[]{:S(2)}) collective-permute-start(f32[136,128]{1,0:T(8,128)S(1)} %get-tuple-element.7), channel_id=1, source_target_pairs={{0,16},{16,0},{1,17},{17,1},{2,18},{18,2},{3,19},{19,3},{4,20},{20... | collective-permute-start | bytes 208904 | tf_op jit(solution)/shard_map/ppermute | solution.py:134
  28.7 3.8 %collective-permute-done.came_ref = f32[136,128]{1,0:T(8,128)S(1)} collective-permute-done((f32[136,128]{1,0:T(8,128)S(1)}, f32[136,128]{1,0:T(8,128)S(1)}, u32[]{:S(2)}, u32[]{:S(2)}) %collective-permute-start) | collective-permute-done | bytes 69664 | tf_op jit(solution)/shard_map/ppermute | solution.py:134
  32.6 0.3 collective-permute-start.3
  32.8 1.2 %collective-permute-start.2 = (f32[136,128]{1,0:T(8,128)S(1)}, f32[136,128]{1,0:T(8,128)S(1)}, u32[]{:S(2)}, u32[]{:S(2)}) collective-permute-start(f32[136,128]{1,0:T(8,128)S(1)} %get-tuple-element.9.refs_0_), channel_id=1, source_target_pairs={{0,2},{1,3},{2,0},{3,1},{4,6},{5,7},{6,4},{7,5},{8,10},{9,11},{10,... | collective-permute-start | bytes 208904 | tf_op jit(solution)/shard_map/ppermute | solution.py:145
  34.1 0.4 collective-permute-start.1
  34.5 10.2 %all_to_all.17 = f32[32,1,128]{2,1,0:T(1,128)S(1)} all-to-all(f32[32,1,128]{2,1,0:T(1,128)S(1)} %bitcast.8), channel_id=1, replica_groups=mesh['far'=2,'near'=4,'rep'=4] {'far','near','rep'}, dimensions={0} | all-to-all | bytes 32768 | tf_op jit(solution)/shard_map/all_to_all | solution.py:146
  44.7 0.0 collective-permute-done.3.refs_3_
  44.7 0.0 collective-permute-done.2.refs_2_
  44.7 0.0 collective-permute-done.1.refs_1_
  44.7 0.8 %scale.1 = (bf16[128,512]{1,0:T(8,128)(2,1)}, bf16[8,512]{1,0:T(8,128)(2,1)}) custom-call(f32[32,128]{1,0:T(8,128)S(1)} %bitcast.7, f32[136,128]{1,0:T(8,128)S(1)} %get-tuple-element.9.refs_0_, f32[136,128]{1,0:T(8,128)S(1)} %collective-permute-done.1.refs_1_, f32[136,128]{1,0:T(8,128)S(1)} %collective-permute-done.2.refs_2_, ...), custom_call_target="tpu_custom_call" | custom-call | tf_op jit(solution)/shard_map/scale/pallas_call | solution.py:147
  (1 shorter events, 0.0 us)
Async XLA Ops:
  0.6 1.2 %copy-start = (bf16[1,1,128,4096]{3,2,1,0:T(8,128)(2,1)S(1)}, bf16[1,1,128,4096]{3,2,1,0:T(8,128)(2,1)}, u32[]{:S(2)}) copy-start(bf16[1,1,128,4096]{3,2,1,0:T(8,128)(2,1)} %param.2) | copy-start | bytes 3145732
  1.9 0.7 %copy-start.1 = (s32[1,1,8,16]{3,2,1,0:T(8,128)S(1)}, s32[1,1,8,16]{3,2,1,0:T(8,128)}, u32[]{:S(2)}) copy-start(s32[1,1,8,16]{3,2,1,0:T(8,128)} %param.3) | copy-start | bytes 1540
  26.0 6.5 %collective-permute-start = (f32[136,128]{1,0:T(8,128)S(1)}, f32[136,128]{1,0:T(8,128)S(1)}, u32[]{:S(2)}, u32[]{:S(2)}) collective-permute-start(f32[136,128]{1,0:T(8,128)S(1)} %get-tuple-element.7), channel_id=1, source_target_pairs={{0,16},{16,0},{1,17},{17,1},{2,18},{18,2},{3,19},{19,3},{4,20},{20... | collective-permute-start | bytes 208904 | tf_op jit(solution)/shard_map/ppermute | solution.py:134
  32.6 12.2 %collective-permute-start.3 = (f32[136,128]{1,0:T(8,128)S(1)}, f32[136,128]{1,0:T(8,128)S(1)}, u32[]{:S(2)}, u32[]{:S(2)}) collective-permute-start(f32[136,128]{1,0:T(8,128)S(1)} %get-tuple-element.9.refs_0_), channel_id=1, source_target_pairs={{0,3},{1,2},{2,1},{3,0},{4,7},{5,6},{6,5},{7,4},{8,11},{9,10},{10,... | collective-permute-start | bytes 208904 | tf_op jit(solution)/shard_map/ppermute | solution.py:145
  32.8 11.9 %collective-permute-start.2 = (f32[136,128]{1,0:T(8,128)S(1)}, f32[136,128]{1,0:T(8,128)S(1)}, u32[]{:S(2)}, u32[]{:S(2)}) collective-permute-start(f32[136,128]{1,0:T(8,128)S(1)} %get-tuple-element.9.refs_0_), channel_id=1, source_target_pairs={{0,2},{1,3},{2,0},{3,1},{4,6},{5,7},{6,4},{7,5},{8,10},{9,11},{10,... | collective-permute-start | bytes 208904 | tf_op jit(solution)/shard_map/ppermute | solution.py:145
  34.1 10.6 %collective-permute-start.1 = (f32[136,128]{1,0:T(8,128)S(1)}, f32[136,128]{1,0:T(8,128)S(1)}, u32[]{:S(2)}, u32[]{:S(2)}) collective-permute-start(f32[136,128]{1,0:T(8,128)S(1)} %get-tuple-element.9.refs_0_), channel_id=1, source_target_pairs={{0,1},{1,0},{2,3},{3,2},{4,5},{5,4},{6,7},{7,6},{8,9},{9,8},{10,11... | collective-permute-start | bytes 208904 | tf_op jit(solution)/shard_map/ppermute | solution.py:145

commit v3 on v2

--- a/solution.py
+++ b/solution.py
@@ -52,13 +52,9 @@
         copy.wait()
 
 
-def sum_kernel(rows, recv_ref, mine_ref, other_ref):
-    parts, held, cols = recv_ref.shape
-    blocks = mine_ref.shape[0] - rows
-    me = lax.axis_index("far")
-    places = (me, 1 - me)
-    totals = [jnp.zeros((rows, cols), jnp.float32)] * 2
-    checks = [jnp.zeros((4 * blocks, cols), jnp.float32)] * 2
+def sum_other_kernel(rows, recv_ref, sums_ref, shares_ref):
+    parts, held, _ = recv_ref.shape
+    blocks = sums_ref.shape[0] - rows
     for part in range(parts):
         weights = recv_ref[part, pl.ds(held - blocks, blocks), :].astype(jnp.float32)
         share = weights / jnp.sum(weights, axis=1, keepdims=True)
@@ -67,16 +63,28 @@
         middle = rest.astype(jnp.bfloat16).astype(jnp.float32)
         low = rest - middle
         terms = jnp.concatenate([high, middle, low, jnp.zeros_like(low)], axis=0)
-        terms = terms.astype(jnp.bfloat16)
-        for i, place in enumerate(places):
-            data = recv_ref[part, pl.ds(pl.multiple_of(place * rows, rows), rows), :]
-            totals[i] += data.astype(jnp.float32)
-            checks[i] += jnp.dot(terms, data, preferred_element_type=jnp.float32)
-    for ref, total, check in zip((mine_ref, other_ref), totals, checks, strict=True):
-        ref[pl.ds(0, rows), :] = total
-        ref[pl.ds(rows, blocks), :] = (
-            check[:blocks] + check[blocks : 2 * blocks] + check[2 * blocks : 3 * blocks]
-        )
+        shares_ref[part] = terms.astype(jnp.bfloat16)
+    add_up(rows, 1 - lax.axis_index("far"), recv_ref, shares_ref, sums_ref)
+
+
+def sum_mine_kernel(rows, recv_ref, shares_ref, sums_ref):
+    add_up(rows, lax.axis_index("far"), recv_ref, shares_ref, sums_ref)
+
+
+def add_up(rows, half, recv_ref, shares_ref, sums_ref):
+    parts, _, cols = recv_ref.shape
+    blocks = sums_ref.shape[0] - rows
+    total = jnp.zeros((rows, cols), jnp.float32)
+    check = jnp.zeros((4 * blocks, cols), jnp.float32)
+    at = pl.ds(pl.multiple_of(half * rows, rows), rows)
+    for part in range(parts):
+        data = recv_ref[part, at, :]
+        total += data.astype(jnp.float32)
+        check += jnp.dot(shares_ref[part], data, preferred_element_type=jnp.float32)
+    sums_ref[pl.ds(0, rows), :] = total
+    sums_ref[pl.ds(rows, blocks), :] = (
+        check[:blocks] + check[blocks : 2 * blocks] + check[2 * blocks : 3 * blocks]
+    )
 
 
 def join_kernel(rows, mine_ref, came_ref, total_ref, square_ref):
@@ -121,17 +129,28 @@
         ],
         compiler_params=GRANT,
         name="pack",
-    )(local, weights)
+    )(
+        pltpu.with_memory_space_constraint(local, pltpu.HBM),
+        pltpu.with_memory_space_constraint(weights, pltpu.HBM),
+    )
     received = lax.all_to_all(packed, ("near", "rep"), 0, 0, tiled=True)
-    mine, other = pl.pallas_call(
-        functools.partial(sum_kernel, rows),
-        out_shape=(sums, sums),
+    other, shares = pl.pallas_call(
+        functools.partial(sum_other_kernel, rows),
+        out_shape=(sums, jax.ShapeDtypeStruct((parts, 4 * blocks, rows), jnp.bfloat16)),
         in_specs=[vmem],
         out_specs=(vmem, vmem),
         compiler_params=GRANT,
-        name="add_up",
+        name="sum_other",
     )(received)
     came = lax.ppermute(other, "far", [(0, 1), (1, 0)])
+    mine = pl.pallas_call(
+        functools.partial(sum_mine_kernel, rows),
+        out_shape=sums,
+        in_specs=[vmem, vmem],
+        out_specs=vmem,
+        compiler_params=GRANT,
+        name="sum_mine",
+    )(received, shares)
     total, square = pl.pallas_call(
         functools.partial(join_kernel, rows),
         out_shape=(sums, jax.ShapeDtypeStruct((far * parts, cols), jnp.float32)),

time: 45.8 us -> 44.6 us (0.974)
  local copies, waits for them, and re-layouts: 1.9 us -> 0 us
  Pallas kernels: 1.73 us -> 2.68 us
    unnamed x4 -> x0, local copies, waits for them, and re-layouts: 1.9 us -> none
    pallas_call x1, Pallas kernels: 0.43 us -> 1.25 us  [small_body(): pl.pallas_call(pack_kernel, out_shape=jax.ShapeDtypeStruct((parts, far *...]
  transfers between devices with their start and end apart: 4 -> 4, of which waited for: 1 -> 1; matrix products, arithmetic and copies ran while one was open for 0% -> 0% of each run, Pallas kernels for 0% -> 1%
where the time goes in v3:
time: 44.6 us; the launch traced here: 44.3 us
  blocking collectives  32.8 us (74%)
  starting transfers between devices  4.58 us (10%)
  waiting for transfers between devices  3.59 us (8%)
  Pallas kernels  2.68 us (6%)
  between operations  0.65 us (1%)
    all_to_all x1, blocking collectives, small_body(): received = lax.all_to_all(packed, ('near', 'rep'), 0, 0, tiled=True)  22.6 us
    all_to_all x1, blocking collectives, small_body(): squares = lax.all_to_all(square, ('far', 'near', 'rep'), 0, 0, tiled=True)  10.2 us
    ppermute x1, waiting for transfers between devices, small_body(): came = lax.ppermute(other, 'far', [(0, 1), (1, 0)])  3.58 us
    ppermute x1, starting transfers between devices, small_body(): came = lax.ppermute(other, 'far', [(0, 1), (1, 0)])  2.65 us
    ppermute x3, starting transfers between devices, small_body(): lax.ppermute(total, 'rep', [(i, i ^ step) for i in range(replicas)])  1.92 us
    pallas_call x1, Pallas kernels, small_body(): pl.pallas_call(pack_kernel, out_shape=jax.ShapeDtypeStruct((parts, far *...  1.25 us
  transfers between devices with their start and end apart: 4, of which 1 were waited for; matrix products, arithmetic and copies ran while one was open for 0% of the time, Pallas kernels for 1%

profile of v3, /device:TPU:0, one launch (start us, length us, event | category | flops | bytes accessed | tf_op | source)
XLA Modules:
  0.0 44.3 jit_solution(12191322033230465117)
XLA Ops:
  0.6 1.3 %pack.1 = bf16[16,264,128]{2,1,0:T(8,128)(2,1)S(1)} custom-call(bf16[128,4096]{1,0:T(8,128)(2,1)} %bitcast.8, s32[8,16]{1,0:T(8,128)} %bitcast.9), custom_call_target="tpu_custom_call" | custom-call | tf_op jit(solution)/shard_map/pack/pallas_call | solution.py:120
  1.9 22.6 %all_to_all.16.recv_ref = bf16[16,264,128]{2,1,0:T(8,128)(2,1)S(1)} all-to-all(bf16[16,264,128]{2,1,0:T(8,128)(2,1)S(1)} %pack.1), channel_id=1, replica_groups=mesh['far'=2,'near'=4,'rep'=4] {'near','rep'}, dimensions={0} | all-to-all | bytes 2162688 | tf_op jit(solution)/shard_map/all_to_all | solution.py:136
  24.5 0.3 sum_other.1
  24.8 2.7 %collective-permute-start = (f32[136,128]{1,0:T(8,128)S(1)}, f32[136,128]{1,0:T(8,128)S(1)}, u32[]{:S(2)}, u32[]{:S(2)}) collective-permute-start(f32[136,128]{1,0:T(8,128)S(1)} %get-tuple-element.7), channel_id=1, source_target_pairs={{0,16},{16,0},{1,17},{17,1},{2,18},{18,2},{3,19},{19,3},{4,20},{20... | collective-permute-start | bytes 208904 | tf_op jit(solution)/shard_map/ppermute | solution.py:145
  27.5 0.2 sum_mine.1.mine_ref
  27.7 3.6 %collective-permute-done.came_ref = f32[136,128]{1,0:T(8,128)S(1)} collective-permute-done((f32[136,128]{1,0:T(8,128)S(1)}, f32[136,128]{1,0:T(8,128)S(1)}, u32[]{:S(2)}, u32[]{:S(2)}) %collective-permute-start) | collective-permute-done | bytes 69664 | tf_op jit(solution)/shard_map/ppermute | solution.py:145
  31.3 0.3 collective-permute-start.3
  31.6 1.2 %collective-permute-start.2 = (f32[136,128]{1,0:T(8,128)S(1)}, f32[136,128]{1,0:T(8,128)S(1)}, u32[]{:S(2)}, u32[]{:S(2)}) collective-permute-start(f32[136,128]{1,0:T(8,128)S(1)} %get-tuple-element.9.refs_0_), channel_id=1, source_target_pairs={{0,2},{1,3},{2,0},{3,1},{4,6},{5,7},{6,4},{7,5},{8,10},{9,11},{10,... | collective-permute-start | bytes 208904 | tf_op jit(solution)/shard_map/ppermute | solution.py:164
  32.9 0.4 collective-permute-start.1
  33.3 10.2 %all_to_all.17 = f32[32,1,128]{2,1,0:T(1,128)S(1)} all-to-all(f32[32,1,128]{2,1,0:T(1,128)S(1)} %bitcast.7), channel_id=1, replica_groups=mesh['far'=2,'near'=4,'rep'=4] {'far','near','rep'}, dimensions={0} | all-to-all | bytes 32768 | tf_op jit(solution)/shard_map/all_to_all | solution.py:165
  43.5 0.0 collective-permute-done.3.refs_3_
  43.5 0.0 collective-permute-done.2.refs_2_
  43.5 0.0 collective-permute-done.1.refs_1_
  43.5 0.8 %scale.1 = (bf16[128,512]{1,0:T(8,128)(2,1)}, bf16[8,512]{1,0:T(8,128)(2,1)}) custom-call(f32[32,128]{1,0:T(8,128)S(1)} %bitcast.6, f32[136,128]{1,0:T(8,128)S(1)} %get-tuple-element.9.refs_0_, f32[136,128]{1,0:T(8,128)S(1)} %collective-permute-done.1.refs_1_, f32[136,128]{1,0:T(8,128)S(1)} %collective-permute-done.2.refs_2_, ...), custom_call_target="tpu_custom_call" | custom-call | tf_op jit(solution)/shard_map/scale/pallas_call | solution.py:166
  (1 shorter events, 0.0 us)
Async XLA Ops:
  24.8 6.5 %collective-permute-start = (f32[136,128]{1,0:T(8,128)S(1)}, f32[136,128]{1,0:T(8,128)S(1)}, u32[]{:S(2)}, u32[]{:S(2)}) collective-permute-start(f32[136,128]{1,0:T(8,128)S(1)} %get-tuple-element.7), channel_id=1, source_target_pairs={{0,16},{16,0},{1,17},{17,1},{2,18},{18,2},{3,19},{19,3},{4,20},{20... | collective-permute-start | bytes 208904 | tf_op jit(solution)/shard_map/ppermute | solution.py:145
  31.3 12.2 %collective-permute-start.3 = (f32[136,128]{1,0:T(8,128)S(1)}, f32[136,128]{1,0:T(8,128)S(1)}, u32[]{:S(2)}, u32[]{:S(2)}) collective-permute-start(f32[136,128]{1,0:T(8,128)S(1)} %get-tuple-element.9.refs_0_), channel_id=1, source_target_pairs={{0,3},{1,2},{2,1},{3,0},{4,7},{5,6},{6,5},{7,4},{8,11},{9,10},{10,... | collective-permute-start | bytes 208904 | tf_op jit(solution)/shard_map/ppermute | solution.py:164
  31.6 11.9 %collective-permute-start.2 = (f32[136,128]{1,0:T(8,128)S(1)}, f32[136,128]{1,0:T(8,128)S(1)}, u32[]{:S(2)}, u32[]{:S(2)}) collective-permute-start(f32[136,128]{1,0:T(8,128)S(1)} %get-tuple-element.9.refs_0_), channel_id=1, source_target_pairs={{0,2},{1,3},{2,0},{3,1},{4,6},{5,7},{6,4},{7,5},{8,10},{9,11},{10,... | collective-permute-start | bytes 208904 | tf_op jit(solution)/shard_map/ppermute | solution.py:164
  32.9 10.6 %collective-permute-start.1 = (f32[136,128]{1,0:T(8,128)S(1)}, f32[136,128]{1,0:T(8,128)S(1)}, u32[]{:S(2)}, u32[]{:S(2)}) collective-permute-start(f32[136,128]{1,0:T(8,128)S(1)} %get-tuple-element.9.refs_0_), channel_id=1, source_target_pairs={{0,1},{1,0},{2,3},{3,2},{4,5},{5,4},{6,7},{7,6},{8,9},{9,8},{10,11... | collective-permute-start | bytes 208904 | tf_op jit(solution)/shard_map/ppermute | solution.py:164

commit v4 on v1

v4 whole, which is shorter than its diff:
```python
import functools

import jax
import jax.numpy as jnp
from jax import lax
from jax.experimental import pallas as pl
from jax.experimental.pallas import tpu as pltpu
from jax.sharding import Mesh
from jax.sharding import PartitionSpec as P

LANES = 128
SUBLANES = 8
FULL = 32767.0
LEAST, MOST = -110, 126
GRANT = pltpu.CompilerParams(vmem_limit_bytes=8 * 1024 * 1024)


def clip_factor(square, total_rows, width):
    return jnp.minimum(
        1.0, 2.0 * jnp.sqrt(jnp.float32(total_rows * width)) / jnp.sqrt(square + 1e-06)
    )


def pack_kernel(mine, grads_hbm, weights_hbm, out_ref, weights_ref, grads_sem, weights_sem):
    core = lax.axis_index("core")
    target = core if mine else 1 - core
    rows, width = grads_hbm.shape
    blocks, block = weights_ref.shape
    cols = out_ref.shape[1]
    chips = width // (4 * cols)
    fetch = pltpu.make_async_copy(weights_hbm, weights_ref, weights_sem)
    fetch.start()
    copies = []
    for chip in range(chips):
        for half in range(2):
            at = pl.multiple_of(((half * chips + chip) * 2 + target) * cols, cols)
            copies.append(
                pltpu.make_async_copy(
                    grads_hbm.at[:, pl.ds(at, cols)],
                    out_ref.at[pl.ds((chip * 2 + half) * rows, rows), :],
                    grads_sem,
                )
            )
            copies[-1].start()
    fetch.wait()
    place = lax.broadcasted_iota(jnp.int32, (block, rows), 1)
    spread = (place % block == lax.broadcasted_iota(jnp.int32, (block, rows), 0)).astype(jnp.bfloat16)
    repeated = jnp.dot(
        weights_ref[...].astype(jnp.bfloat16), spread, preferred_element_type=jnp.float32
    )
    owner = lax.broadcasted_iota(jnp.int32, (blocks, rows), 1) // block
    own = owner == lax.broadcasted_iota(jnp.int32, (blocks, rows), 0)
    out_ref[pl.ds(2 * chips * rows, blocks), :] = jnp.where(own, repeated, 0.0).astype(jnp.bfloat16)
    for copy in copies:
        copy.wait()


def encode(values):
    top = jnp.maximum(jnp.max(jnp.abs(values), axis=0, keepdims=True), 2.0**LEAST)
    power = jnp.clip(jnp.ceil(jnp.log2(top)), float(LEAST), float(MOST))
    codes = jnp.round(values * (jnp.exp2(-power) * FULL))
    return jnp.clip(codes, -FULL, FULL).astype(jnp.int32), power.astype(jnp.int32)


def decode(codes, power):
    return codes.astype(jnp.int32).astype(jnp.float32) * (
        jnp.exp2(power.astype(jnp.float32)) * (1.0 / FULL)
    )


def shares_of(weights):
    weights = weights.astype(jnp.float32)
    share = weights / jnp.sum(weights, axis=1, keepdims=True)
    high = share.astype(jnp.bfloat16).astype(jnp.float32)
    rest = share - high
    middle = rest.astype(jnp.bfloat16).astype(jnp.float32)
    low = rest - middle
    terms = jnp.concatenate([high, middle, low, jnp.zeros_like(low)], axis=0)
    return terms.astype(jnp.bfloat16)


def pair_kernel(rows, mine_ref, came_ref, out_ref):
    chips, held, cols = out_ref.shape
    blocks = mine_ref.shape[0] - 2 * chips * rows
    weights = pl.ds(2 * chips * rows, blocks)
    shares = shares_of(mine_ref[weights, :]), shares_of(came_ref[weights, :])
    for chip in range(chips):
        powers = []
        for half in range(2):
            at = pl.ds((chip * 2 + half) * rows, rows)
            first, second = mine_ref[at, :], came_ref[at, :]
            check = jnp.dot(shares[0], first, preferred_element_type=jnp.float32)
            check += jnp.dot(shares[1], second, preferred_element_type=jnp.float32)
            check = check[:blocks] + check[blocks : 2 * blocks] + check[2 * blocks : 3 * blocks]
            codes, power = encode(first.astype(jnp.float32) + second.astype(jnp.float32))
            out_ref[chip, pl.ds(half * (rows + blocks), rows), :] = codes.astype(jnp.int16)
            powers.append(power)
            codes, power = encode(check)
            out_ref[chip, pl.ds(half * (rows + blocks) + rows, blocks), :] = codes.astype(jnp.int16)
            powers.append(power)
        powers.append(jnp.zeros((SUBLANES - 4, cols), jnp.int32))
        out_ref[chip, pl.ds(held - SUBLANES, SUBLANES), :] = jnp.concatenate(powers, axis=0).astype(
            jnp.int16
        )


def add_up(rows, blocks, half, recv_ref):
    chips, held, cols = recv_ref.shape
    total = jnp.zeros((rows, cols), jnp.float32)
    check = jnp.zeros((blocks, cols), jnp.float32)
    start = pl.multiple_of(half * (rows + blocks), SUBLANES)
    for chip in range(chips):
        powers = recv_ref[chip, pl.ds(held - SUBLANES, SUBLANES), :].astype(jnp.int32)
        powers = jnp.where(half == 0, powers[:2], powers[2:4])
        total += decode(recv_ref[chip, pl.ds(start, rows), :], powers[:1])
        check += decode(recv_ref[chip, pl.ds(start + rows, blocks), :], powers[1:])
    return total, check


def sum_other_kernel(rows, blocks, recv_ref, out_ref):
    total, check = add_up(rows, blocks, 1 - lax.axis_index("far"), recv_ref)
    codes, power = encode(total)
    out_ref[pl.ds(0, rows), :] = codes.astype(jnp.int16)
    codes, check_power = encode(check)
    out_ref[pl.ds(rows, blocks), :] = codes.astype(jnp.int16)
    rest = jnp.zeros((SUBLANES - 2, power.shape[1]), jnp.int32)
    out_ref[pl.ds(rows + blocks, SUBLANES), :] = jnp.concatenate(
        [power, check_power, rest], axis=0
    ).astype(jnp.int16)


def sum_mine_kernel(rows, blocks, recv_ref, sums_ref):
    total, check = add_up(rows, blocks, lax.axis_index("far"), recv_ref)
    sums_ref[pl.ds(0, rows), :] = total
    sums_ref[pl.ds(rows, blocks), :] = check


def join_kernel(rows, blocks, mine_ref, came_ref, total_ref, square_ref):
    powers = came_ref[pl.ds(rows + blocks, SUBLANES), :].astype(jnp.int32)
    total = mine_ref[pl.ds(0, rows), :] + decode(came_ref[pl.ds(0, rows), :], powers[:1])
    total_ref[pl.ds(0, rows), :] = total
    total_ref[pl.ds(rows, blocks), :] = mine_ref[pl.ds(rows, blocks), :] + decode(
        came_ref[pl.ds(rows, blocks), :], powers[1:2]
    )
    square_ref[...] = jnp.broadcast_to(
        jnp.sum(total * total, axis=0, keepdims=True), square_ref.shape
    )


def scale_kernel(rows, width, squares_ref, *refs):
    *total_refs, reduced_ref, check_ref = refs
    cols = total_refs[0].shape[1]
    factor = clip_factor(jnp.sum(squares_ref[...], keepdims=True), rows, width)
    me = lax.axis_index("side") * 2 + lax.axis_index("core")
    for step, total_ref in enumerate(total_refs):
        at = pl.ds(pl.multiple_of((me ^ step) * cols, cols), cols)
        scaled = (total_ref[...] * factor).astype(jnp.bfloat16)
        reduced_ref[:, at] = scaled[:rows]
        check_ref[:, at] = scaled[rows:]


def small_body(sizes, grads, check_weights):
    far, near, side, core = sizes
    local, weights = grads[0, 0], check_weights[0, 0]
    rows, width = local.shape
    blocks = weights.shape[0]
    chips, replicas = near * side, side * core
    cols = width // (far * chips * core)
    vmem = pl.BlockSpec(memory_space=pltpu.VMEM)
    hbm = pl.BlockSpec(memory_space=pltpu.HBM)
    sums = jax.ShapeDtypeStruct((rows + blocks, cols), jnp.float32)
    local = pltpu.with_memory_space_constraint(local, pltpu.HBM)
    weights = pltpu.with_memory_space_constraint(weights, pltpu.HBM)

    def pack(mine):
        return pl.pallas_call(
            functools.partial(pack_kernel, mine),
            out_shape=jax.ShapeDtypeStruct((far * chips * rows + blocks, cols), jnp.bfloat16),
            in_specs=[hbm, hbm],
            out_specs=vmem,
            scratch_shapes=[
                pltpu.VMEM(weights.shape, weights.dtype),
                pltpu.SemaphoreType.DMA,
                pltpu.SemaphoreType.DMA,
            ],
            compiler_params=GRANT,
        )(local, weights)

    def call(kernel, out_shape, *operands):
        return pl.pallas_call(
            kernel,
            out_shape=out_shape,
            in_specs=[vmem] * len(operands),
            out_specs=jax.tree.map(lambda _: vmem, out_shape),
            compiler_params=GRANT,
        )(*operands)

    packed = pack(False)
    came = lax.ppermute(packed, "core", [(0, 1), (1, 0)])
    mine = pack(True)
    coded = call(
        functools.partial(pair_kernel, rows),
        jax.ShapeDtypeStruct((chips, far * (rows + blocks) + SUBLANES, cols), jnp.int16),
        mine,
        came,
    )
    received = lax.all_to_all(coded, ("near", "side"), 0, 0, tiled=True)
    other = call(
        functools.partial(sum_other_kernel, rows, blocks),
        jax.ShapeDtypeStruct((rows + blocks + SUBLANES, cols), jnp.int16),
        received,
    )
    came = lax.ppermute(other, "far", [(0, 1), (1, 0)])
    mine = call(functools.partial(sum_mine_kernel, rows, blocks), sums, received)
    total, square = call(
        functools.partial(join_kernel, rows, blocks),
        (sums, jax.ShapeDtypeStruct((far * chips * core, cols), jnp.float32)),
        mine,
        came,
    )
    totals = [total]
    for step in range(1, replicas):
        swaps = [(i, i ^ step) for i in range(replicas)]
        totals.append(lax.ppermute(total, ("side", "core"), swaps))
    squares = lax.all_to_all(square, ("far", "near", "side", "core"), 0, 0, tiled=True)
    wide = replicas * cols
    return call(
        functools.partial(scale_kernel, rows, width),
        (
            jax.ShapeDtypeStruct((rows, wide), jnp.bfloat16),
            jax.ShapeDtypeStruct((blocks, wide), jnp.bfloat16),
        ),
        squares,
        *totals,
    )


def large_body(grads, check_weights):
    local, weights = grads[0, 0], check_weights[0, 0]
    rows, width = local.shape
    blocks, block = weights.shape
    wsum = jnp.sum(weights, axis=-1).astype(jnp.float32)
    local_check = jnp.einsum(
        "kb,kbe->ke",
        weights.astype(jnp.bfloat16),
        local.reshape(blocks, block, width),
        preferred_element_type=jnp.float32,
    )
    terms = jnp.concatenate([local.astype(jnp.float32), local_check / wsum[:, None]], axis=0)
    owned = lax.psum(lax.psum_scatter(terms, "dp", scatter_dimension=1, tiled=True), "rep")
    square = lax.psum(jnp.sum(owned[:rows] * owned[:rows]), "dp")
    scaled = (clip_factor(square, rows, width) * owned).astype(jnp.bfloat16)
    return scaled[:rows], scaled[rows:]


def solution(mesh):
    replicas, columns = mesh.shape["rep"], mesh.shape["dp"]
    far, near, side, core = sizes = 2, columns // 2, replicas // 2, 2

    def step(grads, check_weights):
        rows, width = grads.shape[2:]
        blocks = check_weights.shape[2]
        tiled = (
            width == columns * replicas * LANES
            and rows == LANES
            and blocks == SUBLANES
            and columns == far * near
            and replicas == side * core
            and replicas & (replicas - 1) == 0
        )
        if tiled:
            axes = ("far", "near", "side", "core")
            body, used = functools.partial(small_body, sizes), Mesh(mesh.devices.reshape(sizes), axes)
            dp, rep = axes[:2], axes[2:]
        else:
            body, used, dp, rep = large_body, mesh, "dp", "rep"
        placed = P(rep, dp, None, None)
        return jax.shard_map(
            body,
            mesh=used,
            in_specs=(placed, placed),
            out_specs=(P(None, dp), P(None, dp)),
            check_vma=False,
        )(grads, check_weights)

    return step
```

time: 51.8 us -> 39 us (0.75)
  blocking collectives: 45.3 us -> 26 us
  starting transfers between devices: 1.93 us -> 5.13 us
  waiting for transfers between devices: 0.01 us -> 3.05 us
  Pallas kernels: 1.7 us -> 3.77 us
  local copies, waits for them, and re-layouts: 1.9 us -> 0 us
    all_to_all x2, blocking collectives: 45.3 us -> 26 us  [the longest x1 16.4 us: small_body(): received = lax.all_to_all(coded, ('near', 'side'), 0, 0, tiled=True)]
    ppermute x3 -> x5, starting transfers between devices: 1.93 us -> 5.13 us  [the longest x1 2.65 us: small_body(): came = lax.ppermute(other, 'far', [(0, 1), (1, 0)])]
    ppermute x3 -> x5, waiting for transfers between devices: 0.01 us -> 3.05 us  [the longest x1 2.58 us: small_body(): came = lax.ppermute(other, 'far', [(0, 1), (1, 0)])]
    pallas_call x3 -> x7, Pallas kernels: 1.7 us -> 3.77 us  [the longest x2 2.15 us: pack(): pl.pallas_call(functools.partial(pack_kernel, mine), out_shape=jax.ShapeD...]
    unnamed x4 -> x0, local copies, waits for them, and re-layouts: 1.9 us -> none
  transfers between devices with their start and end apart: 3 -> 5, of which waited for: 0 -> 2; matrix products, arithmetic and copies ran while one was open for 0% -> 0% of each run, Pallas kernels for 0% -> 3%
where the time goes in v4:
time: 39 us; the launch traced here: 38.6 us
  blocking collectives  26 us (67%)
  starting transfers between devices  5.13 us (13%)
  Pallas kernels  3.77 us (10%)
  waiting for transfers between devices  3.05 us (8%)
  between operations  0.68 us (2%)
    all_to_all x1, blocking collectives, small_body(): received = lax.all_to_all(coded, ('near', 'side'), 0, 0, tiled=True)  16.4 us
    all_to_all x1, blocking collectives, small_body(): lax.all_to_all(square, ('far', 'near', 'side', 'core'), 0, 0, tiled=True)  9.6 us
    ppermute x1, starting transfers between devices, small_body(): came = lax.ppermute(other, 'far', [(0, 1), (1, 0)])  2.65 us
    ppermute x1, waiting for transfers between devices, small_body(): came = lax.ppermute(other, 'far', [(0, 1), (1, 0)])  2.58 us
    pallas_call x2, Pallas kernels, pack(): pl.pallas_call(functools.partial(pack_kernel, mine), out_shape=jax.ShapeD...  2.15 us
    ppermute x3, starting transfers between devices, small_body(): totals.append(lax.ppermute(total, ('side', 'core'), swaps))  1.92 us
    pallas_call x5, Pallas kernels, call(): pl.pallas_call(kernel, out_shape=out_shape, in_specs=[vmem] * len(operand...  1.62 us
  transfers between devices with their start and end apart: 5, of which 2 were waited for; matrix products, arithmetic and copies ran while one was open for 0% of the time, Pallas kernels for 3%

profile of v4, /device:TPU:0, one launch (start us, length us, event | category | flops | bytes accessed | tf_op | source)
XLA Modules:
  0.0 38.6 jit_solution(4548469622075501840)
XLA Ops:
  0.6 1.1 %shard_map.42 = bf16[2056,128]{1,0:T(8,128)(2,1)S(1)} custom-call(bf16[128,4096]{1,0:T(8,128)(2,1)} %bitcast.8, s32[8,16]{1,0:T(8,128)} %bitcast.10), custom_call_target="tpu_custom_call" | custom-call | tf_op jit(solution)/shard_map/pallas_call | solution.py:176
  1.7 0.6 %collective-permute-start = (bf16[2056,128]{1,0:T(8,128)(2,1)S(1)}, bf16[2056,128]{1,0:T(8,128)(2,1)S(1)}, u32[]{:S(2)}, u32[]{:S(2)}) collective-permute-start(bf16[2056,128]{1,0:T(8,128)(2,1)S(1)} %shard_map.42), channel_id=1, source_target_pairs={{0,1},{1,0},{2,3},{3,2},{4,5},{5,4},{6,7},{7,6},{8,9},{9,8},{10,11... | collective-permute-start | bytes 1579016 | tf_op jit(solution)/shard_map/ppermute | solution.py:199
  2.3 1.1 %shard_map.41.mine_ref = bf16[2056,128]{1,0:T(8,128)(2,1)S(1)} custom-call(bf16[128,4096]{1,0:T(8,128)(2,1)} %bitcast.9, s32[8,16]{1,0:T(8,128)} %bitcast.11), custom_call_target="tpu_custom_call" | custom-call | tf_op jit(solution)/shard_map/pallas_call | solution.py:176
  3.4 0.5 %collective-permute-done.came_ref = bf16[2056,128]{1,0:T(8,128)(2,1)S(1)} collective-permute-done((bf16[2056,128]{1,0:T(8,128)(2,1)S(1)}, bf16[2056,128]{1,0:T(8,128)(2,1)S(1)}, u32[]{:S(2)}, u32[]{:S(2)}) %collective-permute-start) | collective-permute-done | bytes 526368 | tf_op jit(solution)/shard_map/ppermute | solution.py:199
  3.8 0.6 %shard_map.43 = s16[8,280,128]{2,1,0:T(8,128)(2,1)S(1)} custom-call(bf16[2056,128]{1,0:T(8,128)(2,1)S(1)} %shard_map.41.mine_ref, bf16[2056,128]{1,0:T(8,128)(2,1)S(1)} %collective-permute-done.came_ref), custom_call_target="tpu_custom_call" | custom-call | tf_op jit(solution)/shard_map/pallas_call | solution.py:190
  4.4 16.4 %all_to_all.16.recv_ref = s16[8,280,128]{2,1,0:T(8,128)(2,1)S(1)} all-to-all(s16[8,280,128]{2,1,0:T(8,128)(2,1)S(1)} %shard_map.43), channel_id=1, replica_groups=mesh['far'=2,'near'=4,'side'=2,'core'=2] {'near','side'}, dimensions={0} | all-to-all | bytes 1146880 | tf_op jit(solution)/shard_map/all_to_all | solution.py:207
  20.8 0.1 shard_map.45
  20.9 2.7 %collective-permute-start.1 = (s16[144,128]{1,0:T(8,128)(2,1)S(1)}, s16[144,128]{1,0:T(8,128)(2,1)S(1)}, u32[]{:S(2)}, u32[]{:S(2)}) collective-permute-start(s16[144,128]{1,0:T(8,128)(2,1)S(1)} %shard_map.45), channel_id=1, source_target_pairs={{0,16},{16,0},{1,17},{17,1},{2,18},{18,2},{3,19},{19,3},{4,20},{20... | collective-permute-start | bytes 110600 | tf_op jit(solution)/shard_map/ppermute | solution.py:213
  23.6 0.1 shard_map.44.mine_ref
  23.7 2.6 %collective-permute-done.1.came_ref = s16[144,128]{1,0:T(8,128)(2,1)S(1)} collective-permute-done((s16[144,128]{1,0:T(8,128)(2,1)S(1)}, s16[144,128]{1,0:T(8,128)(2,1)S(1)}, u32[]{:S(2)}, u32[]{:S(2)}) %collective-permute-start.1) | collective-permute-done | bytes 36896 | tf_op jit(solution)/shard_map/ppermute | solution.py:213
  26.3 0.1 collective-permute-start.4
  26.4 0.6 %collective-permute-start.3 = (f32[136,128]{1,0:T(8,128)S(1)}, f32[136,128]{1,0:T(8,128)S(1)}, u32[]{:S(2)}, u32[]{:S(2)}) collective-permute-start(f32[136,128]{1,0:T(8,128)S(1)} %get-tuple-element.5.refs_0_), channel_id=1, source_target_pairs={{0,2},{1,3},{2,0},{3,1},{4,6},{5,7},{6,4},{7,5},{8,10},{9,11},{10,... | collective-permute-start | bytes 208904 | tf_op jit(solution)/shard_map/ppermute | solution.py:224
  26.9 1.3 %collective-permute-start.2 = (f32[136,128]{1,0:T(8,128)S(1)}, f32[136,128]{1,0:T(8,128)S(1)}, u32[]{:S(2)}, u32[]{:S(2)}) collective-permute-start(f32[136,128]{1,0:T(8,128)S(1)} %get-tuple-element.5.refs_0_), channel_id=1, source_target_pairs={{0,1},{1,0},{2,3},{3,2},{4,5},{5,4},{6,7},{7,6},{8,9},{9,8},{10,11... | collective-permute-start | bytes 208904 | tf_op jit(solution)/shard_map/ppermute | solution.py:224
  28.2 9.6 %all_to_all.17 = f32[32,1,128]{2,1,0:T(1,128)S(1)} all-to-all(f32[32,1,128]{2,1,0:T(1,128)S(1)} %bitcast.7), channel_id=1, replica_groups=mesh['far'=2,'near'=4,'side'=2,'core'=2] {'far','near','side','core'}, dimensions={0} | all-to-all | bytes 32768 | tf_op jit(solution)/shard_map/all_to_all | solution.py:225
  37.8 0.0 collective-permute-done.4.refs_3_
  37.8 0.0 collective-permute-done.3.refs_2_
  37.8 0.0 collective-permute-done.2.refs_1_
  37.8 0.8 %shard_map.47 = (bf16[128,512]{1,0:T(8,128)(2,1)}, bf16[8,512]{1,0:T(8,128)(2,1)}) custom-call(f32[32,128]{1,0:T(8,128)S(1)} %bitcast.6, f32[136,128]{1,0:T(8,128)S(1)} %get-tuple-element.5.refs_0_, f32[136,128]{1,0:T(8,128)S(1)} %collective-permute-done.2.refs_1_, f32[136,128]{1,0:T(8,128)S(1)} %collective-permute-done.3.refs_2_, ...), custom_call_target="tpu_custom_call" | custom-call | tf_op jit(solution)/shard_map/pallas_call | solution.py:190
  (1 shorter events, 0.0 us)
Async XLA Ops:
  1.7 2.1 %collective-permute-start = (bf16[2056,128]{1,0:T(8,128)(2,1)S(1)}, bf16[2056,128]{1,0:T(8,128)(2,1)S(1)}, u32[]{:S(2)}, u32[]{:S(2)}) collective-permute-start(bf16[2056,128]{1,0:T(8,128)(2,1)S(1)} %shard_map.42), channel_id=1, source_target_pairs={{0,1},{1,0},{2,3},{3,2},{4,5},{5,4},{6,7},{7,6},{8,9},{9,8},{10,11... | collective-permute-start | bytes 1579016 | tf_op jit(solution)/shard_map/ppermute | solution.py:199
  20.9 5.3 %collective-permute-start.1 = (s16[144,128]{1,0:T(8,128)(2,1)S(1)}, s16[144,128]{1,0:T(8,128)(2,1)S(1)}, u32[]{:S(2)}, u32[]{:S(2)}) collective-permute-start(s16[144,128]{1,0:T(8,128)(2,1)S(1)} %shard_map.45), channel_id=1, source_target_pairs={{0,16},{16,0},{1,17},{17,1},{2,18},{18,2},{3,19},{19,3},{4,20},{20... | collective-permute-start | bytes 110600 | tf_op jit(solution)/shard_map/ppermute | solution.py:213
  26.3 11.5 %collective-permute-start.4 = (f32[136,128]{1,0:T(8,128)S(1)}, f32[136,128]{1,0:T(8,128)S(1)}, u32[]{:S(2)}, u32[]{:S(2)}) collective-permute-start(f32[136,128]{1,0:T(8,128)S(1)} %get-tuple-element.5.refs_0_), channel_id=1, source_target_pairs={{0,3},{1,2},{2,1},{3,0},{4,7},{5,6},{6,5},{7,4},{8,11},{9,10},{10,... | collective-permute-start | bytes 208904 | tf_op jit(solution)/shard_map/ppermute | solution.py:224
  26.4 11.5 %collective-permute-start.3 = (f32[136,128]{1,0:T(8,128)S(1)}, f32[136,128]{1,0:T(8,128)S(1)}, u32[]{:S(2)}, u32[]{:S(2)}) collective-permute-start(f32[136,128]{1,0:T(8,128)S(1)} %get-tuple-element.5.refs_0_), channel_id=1, source_target_pairs={{0,2},{1,3},{2,0},{3,1},{4,6},{5,7},{6,4},{7,5},{8,10},{9,11},{10,... | collective-permute-start | bytes 208904 | tf_op jit(solution)/shard_map/ppermute | solution.py:224
  26.9 10.9 %collective-permute-start.2 = (f32[136,128]{1,0:T(8,128)S(1)}, f32[136,128]{1,0:T(8,128)S(1)}, u32[]{:S(2)}, u32[]{:S(2)}) collective-permute-start(f32[136,128]{1,0:T(8,128)S(1)} %get-tuple-element.5.refs_0_), channel_id=1, source_target_pairs={{0,1},{1,0},{2,3},{3,2},{4,5},{5,4},{6,7},{7,6},{8,9},{9,8},{10,11... | collective-permute-start | bytes 208904 | tf_op jit(solution)/shard_map/ppermute | solution.py:224

commit v5 on v4

--- a/solution.py
+++ b/solution.py
@@ -11,7 +11,7 @@
 LANES = 128
 SUBLANES = 8
 FULL = 32767.0
-LEAST, MOST = -110, 126
+LEAST, MOST = -126, 126
 GRANT = pltpu.CompilerParams(vmem_limit_bytes=8 * 1024 * 1024)
 
 
@@ -58,14 +58,13 @@
 def encode(values):
     top = jnp.maximum(jnp.max(jnp.abs(values), axis=0, keepdims=True), 2.0**LEAST)
     power = jnp.clip(jnp.ceil(jnp.log2(top)), float(LEAST), float(MOST))
-    codes = jnp.round(values * (jnp.exp2(-power) * FULL))
+    codes = jnp.round(values * jnp.exp2(-power) * FULL)
     return jnp.clip(codes, -FULL, FULL).astype(jnp.int32), power.astype(jnp.int32)
 
 
 def decode(codes, power):
-    return codes.astype(jnp.int32).astype(jnp.float32) * (
-        jnp.exp2(power.astype(jnp.float32)) * (1.0 / FULL)
-    )
+    values = codes.astype(jnp.int32).astype(jnp.float32) * (1.0 / FULL)
+    return values * jnp.exp2(power.astype(jnp.float32))
 
 
 def shares_of(weights):

time: 39 us -> 39 us (level)
  no operation moved by 1% of the time
where the time goes in v5:
time: 39 us; the launch traced here: 38.7 us
  blocking collectives  26 us (67%)
  starting transfers between devices  5.12 us (13%)
  Pallas kernels  3.84 us (10%)
  waiting for transfers between devices  3.03 us (8%)
  between operations  0.68 us (2%)
    all_to_all x1, blocking collectives, small_body(): received = lax.all_to_all(coded, ('near', 'side'), 0, 0, tiled=True)  16.4 us
    all_to_all x1, blocking collectives, small_body(): lax.all_to_all(square, ('far', 'near', 'side', 'core'), 0, 0, tiled=True)  9.6 us
    ppermute x1, starting transfers between devices, small_body(): came = lax.ppermute(other, 'far', [(0, 1), (1, 0)])  2.65 us
    ppermute x1, waiting for transfers between devices, small_body(): came = lax.ppermute(other, 'far', [(0, 1), (1, 0)])  2.56 us
    pallas_call x2, Pallas kernels, pack(): pl.pallas_call(functools.partial(pack_kernel, mine), out_shape=jax.ShapeD...  2.15 us
    ppermute x3, starting transfers between devices, small_body(): totals.append(lax.ppermute(total, ('side', 'core'), swaps))  1.91 us
    pallas_call x5, Pallas kernels, call(): pl.pallas_call(kernel, out_shape=out_shape, in_specs=[vmem] * len(operand...  1.69 us
  transfers between devices with their start and end apart: 5, of which 2 were waited for; matrix products, arithmetic and copies ran while one was open for 0% of the time, Pallas kernels for 3%

profile of v5, /device:TPU:0, one launch (start us, length us, event | category | flops | bytes accessed | tf_op | source)
XLA Modules:
  0.0 38.7 jit_solution(17903284207156714975)
XLA Ops:
  0.6 1.1 %shard_map.42 = bf16[2056,128]{1,0:T(8,128)(2,1)S(1)} custom-call(bf16[128,4096]{1,0:T(8,128)(2,1)} %bitcast.8, s32[8,16]{1,0:T(8,128)} %bitcast.10), custom_call_target="tpu_custom_call" | custom-call | tf_op jit(solution)/shard_map/pallas_call | solution.py:175
  1.7 0.6 %collective-permute-start = (bf16[2056,128]{1,0:T(8,128)(2,1)S(1)}, bf16[2056,128]{1,0:T(8,128)(2,1)S(1)}, u32[]{:S(2)}, u32[]{:S(2)}) collective-permute-start(bf16[2056,128]{1,0:T(8,128)(2,1)S(1)} %shard_map.42), channel_id=1, source_target_pairs={{0,1},{1,0},{2,3},{3,2},{4,5},{5,4},{6,7},{7,6},{8,9},{9,8},{10,11... | collective-permute-start | bytes 1579016 | tf_op jit(solution)/shard_map/ppermute | solution.py:198
  2.3 1.1 %shard_map.41.mine_ref = bf16[2056,128]{1,0:T(8,128)(2,1)S(1)} custom-call(bf16[128,4096]{1,0:T(8,128)(2,1)} %bitcast.9, s32[8,16]{1,0:T(8,128)} %bitcast.11), custom_call_target="tpu_custom_call" | custom-call | tf_op jit(solution)/shard_map/pallas_call | solution.py:175
  3.4 0.5 %collective-permute-done.came_ref = bf16[2056,128]{1,0:T(8,128)(2,1)S(1)} collective-permute-done((bf16[2056,128]{1,0:T(8,128)(2,1)S(1)}, bf16[2056,128]{1,0:T(8,128)(2,1)S(1)}, u32[]{:S(2)}, u32[]{:S(2)}) %collective-permute-start) | collective-permute-done | bytes 526368 | tf_op jit(solution)/shard_map/ppermute | solution.py:198
  3.8 0.6 %shard_map.43 = s16[8,280,128]{2,1,0:T(8,128)(2,1)S(1)} custom-call(bf16[2056,128]{1,0:T(8,128)(2,1)S(1)} %shard_map.41.mine_ref, bf16[2056,128]{1,0:T(8,128)(2,1)S(1)} %collective-permute-done.came_ref), custom_call_target="tpu_custom_call" | custom-call | tf_op jit(solution)/shard_map/pallas_call | solution.py:189
  4.4 16.4 %all_to_all.16.recv_ref = s16[8,280,128]{2,1,0:T(8,128)(2,1)S(1)} all-to-all(s16[8,280,128]{2,1,0:T(8,128)(2,1)S(1)} %shard_map.43), channel_id=1, replica_groups=mesh['far'=2,'near'=4,'side'=2,'core'=2] {'near','side'}, dimensions={0} | all-to-all | bytes 1146880 | tf_op jit(solution)/shard_map/all_to_all | solution.py:206
  20.8 0.1 shard_map.45
  21.0 2.7 %collective-permute-start.1 = (s16[144,128]{1,0:T(8,128)(2,1)S(1)}, s16[144,128]{1,0:T(8,128)(2,1)S(1)}, u32[]{:S(2)}, u32[]{:S(2)}) collective-permute-start(s16[144,128]{1,0:T(8,128)(2,1)S(1)} %shard_map.45), channel_id=1, source_target_pairs={{0,16},{16,0},{1,17},{17,1},{2,18},{18,2},{3,19},{19,3},{4,20},{20... | collective-permute-start | bytes 110600 | tf_op jit(solution)/shard_map/ppermute | solution.py:212
  23.6 0.1 shard_map.44.mine_ref
  23.7 2.6 %collective-permute-done.1.came_ref = s16[144,128]{1,0:T(8,128)(2,1)S(1)} collective-permute-done((s16[144,128]{1,0:T(8,128)(2,1)S(1)}, s16[144,128]{1,0:T(8,128)(2,1)S(1)}, u32[]{:S(2)}, u32[]{:S(2)}) %collective-permute-start.1) | collective-permute-done | bytes 36896 | tf_op jit(solution)/shard_map/ppermute | solution.py:212
  26.3 0.1 collective-permute-start.4
  26.4 0.6 %collective-permute-start.3 = (f32[136,128]{1,0:T(8,128)S(1)}, f32[136,128]{1,0:T(8,128)S(1)}, u32[]{:S(2)}, u32[]{:S(2)}) collective-permute-start(f32[136,128]{1,0:T(8,128)S(1)} %get-tuple-element.5.refs_0_), channel_id=1, source_target_pairs={{0,2},{1,3},{2,0},{3,1},{4,6},{5,7},{6,4},{7,5},{8,10},{9,11},{10,... | collective-permute-start | bytes 208904 | tf_op jit(solution)/shard_map/ppermute | solution.py:223
  27.0 1.3 %collective-permute-start.2 = (f32[136,128]{1,0:T(8,128)S(1)}, f32[136,128]{1,0:T(8,128)S(1)}, u32[]{:S(2)}, u32[]{:S(2)}) collective-permute-start(f32[136,128]{1,0:T(8,128)S(1)} %get-tuple-element.5.refs_0_), channel_id=1, source_target_pairs={{0,1},{1,0},{2,3},{3,2},{4,5},{5,4},{6,7},{7,6},{8,9},{9,8},{10,11... | collective-permute-start | bytes 208904 | tf_op jit(solution)/shard_map/ppermute | solution.py:223
  28.3 9.6 %all_to_all.17 = f32[32,1,128]{2,1,0:T(1,128)S(1)} all-to-all(f32[32,1,128]{2,1,0:T(1,128)S(1)} %bitcast.7), channel_id=1, replica_groups=mesh['far'=2,'near'=4,'side'=2,'core'=2] {'far','near','side','core'}, dimensions={0} | all-to-all | bytes 32768 | tf_op jit(solution)/shard_map/all_to_all | solution.py:224
  37.9 0.0 collective-permute-done.4.refs_3_
  37.9 0.0 collective-permute-done.3.refs_2_
  37.9 0.0 collective-permute-done.2.refs_1_
  37.9 0.8 %shard_map.47 = (bf16[128,512]{1,0:T(8,128)(2,1)}, bf16[8,512]{1,0:T(8,128)(2,1)}) custom-call(f32[32,128]{1,0:T(8,128)S(1)} %bitcast.6, f32[136,128]{1,0:T(8,128)S(1)} %get-tuple-element.5.refs_0_, f32[136,128]{1,0:T(8,128)S(1)} %collective-permute-done.2.refs_1_, f32[136,128]{1,0:T(8,128)S(1)} %collective-permute-done.3.refs_2_, ...), custom_call_target="tpu_custom_call" | custom-call | tf_op jit(solution)/shard_map/pallas_call | solution.py:189
  (1 shorter events, 0.0 us)
Async XLA Ops:
  1.7 2.1 %collective-permute-start = (bf16[2056,128]{1,0:T(8,128)(2,1)S(1)}, bf16[2056,128]{1,0:T(8,128)(2,1)S(1)}, u32[]{:S(2)}, u32[]{:S(2)}) collective-permute-start(bf16[2056,128]{1,0:T(8,128)(2,1)S(1)} %shard_map.42), channel_id=1, source_target_pairs={{0,1},{1,0},{2,3},{3,2},{4,5},{5,4},{6,7},{7,6},{8,9},{9,8},{10,11... | collective-permute-start | bytes 1579016 | tf_op jit(solution)/shard_map/ppermute | solution.py:198
  21.0 5.3 %collective-permute-start.1 = (s16[144,128]{1,0:T(8,128)(2,1)S(1)}, s16[144,128]{1,0:T(8,128)(2,1)S(1)}, u32[]{:S(2)}, u32[]{:S(2)}) collective-permute-start(s16[144,128]{1,0:T(8,128)(2,1)S(1)} %shard_map.45), channel_id=1, source_target_pairs={{0,16},{16,0},{1,17},{17,1},{2,18},{18,2},{3,19},{19,3},{4,20},{20... | collective-permute-start | bytes 110600 | tf_op jit(solution)/shard_map/ppermute | solution.py:212
  26.3 11.5 %collective-permute-start.4 = (f32[136,128]{1,0:T(8,128)S(1)}, f32[136,128]{1,0:T(8,128)S(1)}, u32[]{:S(2)}, u32[]{:S(2)}) collective-permute-start(f32[136,128]{1,0:T(8,128)S(1)} %get-tuple-element.5.refs_0_), channel_id=1, source_target_pairs={{0,3},{1,2},{2,1},{3,0},{4,7},{5,6},{6,5},{7,4},{8,11},{9,10},{10,... | collective-permute-start | bytes 208904 | tf_op jit(solution)/shard_map/ppermute | solution.py:223
  26.4 11.5 %collective-permute-start.3 = (f32[136,128]{1,0:T(8,128)S(1)}, f32[136,128]{1,0:T(8,128)S(1)}, u32[]{:S(2)}, u32[]{:S(2)}) collective-permute-start(f32[136,128]{1,0:T(8,128)S(1)} %get-tuple-element.5.refs_0_), channel_id=1, source_target_pairs={{0,2},{1,3},{2,0},{3,1},{4,6},{5,7},{6,4},{7,5},{8,10},{9,11},{10,... | collective-permute-start | bytes 208904 | tf_op jit(solution)/shard_map/ppermute | solution.py:223
  27.0 10.9 %collective-permute-start.2 = (f32[136,128]{1,0:T(8,128)S(1)}, f32[136,128]{1,0:T(8,128)S(1)}, u32[]{:S(2)}, u32[]{:S(2)}) collective-permute-start(f32[136,128]{1,0:T(8,128)S(1)} %get-tuple-element.5.refs_0_), channel_id=1, source_target_pairs={{0,1},{1,0},{2,3},{3,2},{4,5},{5,4},{6,7},{7,6},{8,9},{9,8},{10,11... | collective-permute-start | bytes 208904 | tf_op jit(solution)/shard_map/ppermute | solution.py:223

commit v6 on v5

--- a/solution.py
+++ b/solution.py
@@ -92,13 +92,13 @@
             check += jnp.dot(shares[1], second, preferred_element_type=jnp.float32)
             check = check[:blocks] + check[blocks : 2 * blocks] + check[2 * blocks : 3 * blocks]
             codes, power = encode(first.astype(jnp.float32) + second.astype(jnp.float32))
-            out_ref[chip, pl.ds(half * (rows + blocks), rows), :] = codes.astype(jnp.int16)
+            out_ref[chips - 1 - chip, pl.ds(half * (rows + blocks), rows), :] = codes.astype(jnp.int16)
             powers.append(power)
             codes, power = encode(check)
-            out_ref[chip, pl.ds(half * (rows + blocks) + rows, blocks), :] = codes.astype(jnp.int16)
+            out_ref[chips - 1 - chip, pl.ds(half * (rows + blocks) + rows, blocks), :] = codes.astype(jnp.int16)
             powers.append(power)
         powers.append(jnp.zeros((SUBLANES - 4, cols), jnp.int32))
-        out_ref[chip, pl.ds(held - SUBLANES, SUBLANES), :] = jnp.concatenate(powers, axis=0).astype(
+        out_ref[chips - 1 - chip, pl.ds(held - SUBLANES, SUBLANES), :] = jnp.concatenate(powers, axis=0).astype(
             jnp.int16
         )
 
@@ -116,33 +116,34 @@
     return total, check
 
 
-def sum_other_kernel(rows, blocks, recv_ref, out_ref):
-    total, check = add_up(rows, blocks, 1 - lax.axis_index("far"), recv_ref)
-    codes, power = encode(total)
-    out_ref[pl.ds(0, rows), :] = codes.astype(jnp.int16)
-    codes, check_power = encode(check)
-    out_ref[pl.ds(rows, blocks), :] = codes.astype(jnp.int16)
-    rest = jnp.zeros((SUBLANES - 2, power.shape[1]), jnp.int32)
-    out_ref[pl.ds(rows + blocks, SUBLANES), :] = jnp.concatenate(
-        [power, check_power, rest], axis=0
-    ).astype(jnp.int16)
-
-
-def sum_mine_kernel(rows, blocks, recv_ref, sums_ref):
-    total, check = add_up(rows, blocks, lax.axis_index("far"), recv_ref)
-    sums_ref[pl.ds(0, rows), :] = total
-    sums_ref[pl.ds(rows, blocks), :] = check
-
-
-def join_kernel(rows, blocks, mine_ref, came_ref, total_ref, square_ref):
-    powers = came_ref[pl.ds(rows + blocks, SUBLANES), :].astype(jnp.int32)
+def sum_kernel(rows, blocks, recv_ref, out_ref, mine_ref, other_ref):
+    far = lax.axis_index("far")
+    other, other_check = add_up(rows, blocks, 1 - far, recv_ref)
+    mine, mine_check = add_up(rows, blocks, far, recv_ref)
+    powers, start = [], 0
+    for values in (other, other_check, mine):
+        codes, power = encode(values)
+        out_ref[pl.ds(start, values.shape[0]), :] = codes.astype(jnp.int16)
+        powers.append(power)
+        start += values.shape[0]
+    powers.append(jnp.zeros((SUBLANES - len(powers), out_ref.shape[1]), jnp.int32))
+    out_ref[pl.ds(start, SUBLANES), :] = jnp.concatenate(powers, axis=0).astype(jnp.int16)
+    mine_ref[pl.ds(0, rows), :] = mine
+    mine_ref[pl.ds(rows, blocks), :] = mine_check
+    other_ref[...] = other
+
+
+def join_kernel(rows, blocks, mine_ref, other_ref, came_ref, total_ref, square_ref):
+    held = rows + blocks
+    powers = came_ref[pl.ds(held + rows, SUBLANES), :].astype(jnp.int32)
     total = mine_ref[pl.ds(0, rows), :] + decode(came_ref[pl.ds(0, rows), :], powers[:1])
+    other = other_ref[...] + decode(came_ref[pl.ds(held, rows), :], powers[2:3])
+    square_ref[...] = jnp.broadcast_to(
+        jnp.sum(total * total + other * other, axis=0, keepdims=True), square_ref.shape
+    )
     total_ref[pl.ds(0, rows), :] = total
     total_ref[pl.ds(rows, blocks), :] = mine_ref[pl.ds(rows, blocks), :] + decode(
         came_ref[pl.ds(rows, blocks), :], powers[1:2]
-    )
-    square_ref[...] = jnp.broadcast_to(
-        jnp.sum(total * total, axis=0, keepdims=True), square_ref.shape
     )
 
 
@@ -203,25 +204,32 @@
         mine,
         came,
     )
-    received = lax.all_to_all(coded, ("near", "side"), 0, 0, tiled=True)
-    other = call(
-        functools.partial(sum_other_kernel, rows, blocks),
-        jax.ShapeDtypeStruct((rows + blocks + SUBLANES, cols), jnp.int16),
+    backward = [list(range(chips))[::-1]]
+    received = lax.all_to_all(
+        coded, ("near", "side"), 0, 0, tiled=True, axis_index_groups=backward
+    )
+    part = jax.ShapeDtypeStruct((rows, cols), jnp.float32)
+    codes, mine, other = call(
+        functools.partial(sum_kernel, rows, blocks),
+        (jax.ShapeDtypeStruct((2 * rows + blocks + SUBLANES, cols), jnp.int16), sums, part),
         received,
     )
-    came = lax.ppermute(other, "far", [(0, 1), (1, 0)])
-    mine = call(functools.partial(sum_mine_kernel, rows, blocks), sums, received)
+    came = lax.ppermute(codes, "far", [(0, 1), (1, 0)])
     total, square = call(
         functools.partial(join_kernel, rows, blocks),
-        (sums, jax.ShapeDtypeStruct((far * chips * core, cols), jnp.float32)),
+        (sums, jax.ShapeDtypeStruct((chips * core, cols), jnp.float32)),
         mine,
+        other,
         came,
     )
     totals = [total]
     for step in range(1, replicas):
         swaps = [(i, i ^ step) for i in range(replicas)]
         totals.append(lax.ppermute(total, ("side", "core"), swaps))
-    squares = lax.all_to_all(square, ("far", "near", "side", "core"), 0, 0, tiled=True)
+    backward = [list(range(chips * core))[::-1]]
+    squares = lax.all_to_all(
+        square, ("near", "side", "core"), 0, 0, tiled=True, axis_index_groups=backward
+    )
     wide = replicas * cols
     return call(
         functools.partial(scale_kernel, rows, width),

time: 39 us -> 36 us (0.923)
  blocking collectives: 26 us -> 22.7 us
    all_to_all x2, blocking collectives: 26 us -> 22.7 us  [the longest x1 14.8 us: small_body(): lax.all_to_all(coded, ('near', 'side'), 0, 0, tiled=True, axis_index_grou...]
    pallas_call x5 -> x4, Pallas kernels: 1.69 us -> 1.71 us  [call(): pl.pallas_call(kernel, out_shape=out_shape, in_specs=[vmem] * len(operand...]
where the time goes in v6:
time: 36 us; the launch traced here: 35.6 us
  blocking collectives  22.7 us (63%)
  starting transfers between devices  5.13 us (14%)
  Pallas kernels  3.86 us (11%)
  waiting for transfers between devices  3.24 us (9%)
  between operations  0.67 us (2%)
    all_to_all x1, blocking collectives, small_body(): lax.all_to_all(coded, ('near', 'side'), 0, 0, tiled=True, axis_index_grou...  14.8 us
    all_to_all x1, blocking collectives, small_body(): lax.all_to_all(square, ('near', 'side', 'core'), 0, 0, tiled=True, axis_i...  7.92 us
    ppermute x1, waiting for transfers between devices, small_body(): came = lax.ppermute(codes, 'far', [(0, 1), (1, 0)])  2.77 us
    ppermute x1, starting transfers between devices, small_body(): came = lax.ppermute(codes, 'far', [(0, 1), (1, 0)])  2.65 us
    pallas_call x2, Pallas kernels, pack(): pl.pallas_call(functools.partial(pack_kernel, mine), out_shape=jax.ShapeD...  2.15 us
    ppermute x3, starting transfers between devices, small_body(): totals.append(lax.ppermute(total, ('side', 'core'), swaps))  1.92 us
    pallas_call x4, Pallas kernels, call(): pl.pallas_call(kernel, out_shape=out_shape, in_specs=[vmem] * len(operand...  1.71 us
  transfers between devices with their start and end apart: 5, of which 2 were waited for; matrix products, arithmetic and copies ran while one was open for 0% of the time, Pallas kernels for 3%

profile of v6, /device:TPU:0, one launch (start us, length us, event | category | flops | bytes accessed | tf_op | source)
XLA Modules:
  0.0 35.6 jit_solution(6324712856873636726)
XLA Ops:
  0.6 1.1 %shard_map.42 = bf16[2056,128]{1,0:T(8,128)(2,1)S(1)} custom-call(bf16[128,4096]{1,0:T(8,128)(2,1)} %bitcast.8, s32[8,16]{1,0:T(8,128)} %bitcast.10), custom_call_target="tpu_custom_call" | custom-call | tf_op jit(solution)/shard_map/pallas_call | solution.py:176
  1.7 0.6 %collective-permute-start = (bf16[2056,128]{1,0:T(8,128)(2,1)S(1)}, bf16[2056,128]{1,0:T(8,128)(2,1)S(1)}, u32[]{:S(2)}, u32[]{:S(2)}) collective-permute-start(bf16[2056,128]{1,0:T(8,128)(2,1)S(1)} %shard_map.42), channel_id=1, source_target_pairs={{0,1},{1,0},{2,3},{3,2},{4,5},{5,4},{6,7},{7,6},{8,9},{9,8},{10,11... | collective-permute-start | bytes 1579016 | tf_op jit(solution)/shard_map/ppermute | solution.py:199
  2.3 1.1 %shard_map.41.mine_ref = bf16[2056,128]{1,0:T(8,128)(2,1)S(1)} custom-call(bf16[128,4096]{1,0:T(8,128)(2,1)} %bitcast.9, s32[8,16]{1,0:T(8,128)} %bitcast.11), custom_call_target="tpu_custom_call" | custom-call | tf_op jit(solution)/shard_map/pallas_call | solution.py:176
  3.4 0.5 %collective-permute-done.came_ref = bf16[2056,128]{1,0:T(8,128)(2,1)S(1)} collective-permute-done((bf16[2056,128]{1,0:T(8,128)(2,1)S(1)}, bf16[2056,128]{1,0:T(8,128)(2,1)S(1)}, u32[]{:S(2)}, u32[]{:S(2)}) %collective-permute-start) | collective-permute-done | bytes 526368 | tf_op jit(solution)/shard_map/ppermute | solution.py:199
  3.8 0.6 %shard_map.43 = s16[8,280,128]{2,1,0:T(8,128)(2,1)S(1)} custom-call(bf16[2056,128]{1,0:T(8,128)(2,1)S(1)} %shard_map.41.mine_ref, bf16[2056,128]{1,0:T(8,128)(2,1)S(1)} %collective-permute-done.came_ref), custom_call_target="tpu_custom_call" | custom-call | tf_op jit(solution)/shard_map/pallas_call | solution.py:190
  4.4 14.8 %all_to_all.16.recv_ref = s16[8,280,128]{2,1,0:T(8,128)(2,1)S(1)} all-to-all(s16[8,280,128]{2,1,0:T(8,128)(2,1)S(1)} %shard_map.43), channel_id=1, replica_groups={{14,12,10,8,6,4,2,0},{15,13,11,9,7,5,3,1},{30,28,26,24,22,20,18,16},{31..., dimensions={0} | all-to-all | bytes 1146880 | tf_op jit(solution)/shard_map/all_to_all | solution.py:208
  19.2 0.3 shard_map.44
  19.5 2.7 %collective-permute-start.1 = (s16[272,128]{1,0:T(8,128)(2,1)S(1)}, s16[272,128]{1,0:T(8,128)(2,1)S(1)}, u32[]{:S(2)}, u32[]{:S(2)}) collective-permute-start(s16[272,128]{1,0:T(8,128)(2,1)S(1)} %get-tuple-element.9), channel_id=1, source_target_pairs={{0,16},{16,0},{1,17},{17,1},{2,18},{18,2},{3,19},{19,3},{4,20},{20... | collective-permute-start | bytes 208904 | tf_op jit(solution)/shard_map/ppermute | solution.py:217
  22.1 2.8 %collective-permute-done.1.came_ref = s16[272,128]{1,0:T(8,128)(2,1)S(1)} collective-permute-done((s16[272,128]{1,0:T(8,128)(2,1)S(1)}, s16[272,128]{1,0:T(8,128)(2,1)S(1)}, u32[]{:S(2)}, u32[]{:S(2)}) %collective-permute-start.1) | collective-permute-done | bytes 69664 | tf_op jit(solution)/shard_map/ppermute | solution.py:217
  25.0 0.6 %collective-permute-start.4 = (f32[136,128]{1,0:T(8,128)S(1)}, f32[136,128]{1,0:T(8,128)S(1)}, u32[]{:S(2)}, u32[]{:S(2)}) collective-permute-start(f32[136,128]{1,0:T(8,128)S(1)} %get-tuple-element.11.refs_0_), channel_id=1, source_target_pairs={{0,3},{1,2},{2,1},{3,0},{4,7},{5,6},{6,5},{7,4},{8,11},{9,10},{10,... | collective-permute-start | bytes 208904 | tf_op jit(solution)/shard_map/ppermute | solution.py:228
  25.6 1.0 %collective-permute-start.3 = (f32[136,128]{1,0:T(8,128)S(1)}, f32[136,128]{1,0:T(8,128)S(1)}, u32[]{:S(2)}, u32[]{:S(2)}) collective-permute-start(f32[136,128]{1,0:T(8,128)S(1)} %get-tuple-element.11.refs_0_), channel_id=1, source_target_pairs={{0,2},{1,3},{2,0},{3,1},{4,6},{5,7},{6,4},{7,5},{8,10},{9,11},{10,... | collective-permute-start | bytes 208904 | tf_op jit(solution)/shard_map/ppermute | solution.py:228
  26.6 0.3 collective-permute-start.2
  26.9 7.9 %all_to_all.17 = f32[16,1,128]{2,1,0:T(1,128)S(1)} all-to-all(f32[16,1,128]{2,1,0:T(1,128)S(1)} %bitcast.7), channel_id=1, replica_groups={{15,14,13,12,11,10,9,8,7,6,5,4,3,2,1,0},{31,30,29,28,27,26,25,24,23,22,..., dimensions={0} | all-to-all | bytes 16384 | tf_op jit(solution)/shard_map/all_to_all | solution.py:230
  34.8 0.0 collective-permute-done.4.refs_3_
  34.8 0.0 collective-permute-done.3.refs_2_
  34.8 0.0 collective-permute-done.2.refs_1_
  34.8 0.8 %shard_map.46 = (bf16[128,512]{1,0:T(8,128)(2,1)}, bf16[8,512]{1,0:T(8,128)(2,1)}) custom-call(f32[16,128]{1,0:T(8,128)S(1)} %bitcast.6, f32[136,128]{1,0:T(8,128)S(1)} %get-tuple-element.11.refs_0_, f32[136,128]{1,0:T(8,128)S(1)} %collective-permute-done.2.refs_1_, f32[136,128]{1,0:T(8,128)S(1)} %collective-permute-done.3.refs_2_, ...), custom_call_target="tpu_custom_call" | custom-call | tf_op jit(solution)/shard_map/pallas_call | solution.py:190
  (1 shorter events, 0.0 us)
Async XLA Ops:
  1.7 2.1 %collective-permute-start = (bf16[2056,128]{1,0:T(8,128)(2,1)S(1)}, bf16[2056,128]{1,0:T(8,128)(2,1)S(1)}, u32[]{:S(2)}, u32[]{:S(2)}) collective-permute-start(bf16[2056,128]{1,0:T(8,128)(2,1)S(1)} %shard_map.42), channel_id=1, source_target_pairs={{0,1},{1,0},{2,3},{3,2},{4,5},{5,4},{6,7},{7,6},{8,9},{9,8},{10,11... | collective-permute-start | bytes 1579016 | tf_op jit(solution)/shard_map/ppermute | solution.py:199
  19.5 5.4 %collective-permute-start.1 = (s16[272,128]{1,0:T(8,128)(2,1)S(1)}, s16[272,128]{1,0:T(8,128)(2,1)S(1)}, u32[]{:S(2)}, u32[]{:S(2)}) collective-permute-start(s16[272,128]{1,0:T(8,128)(2,1)S(1)} %get-tuple-element.9), channel_id=1, source_target_pairs={{0,16},{16,0},{1,17},{17,1},{2,18},{18,2},{3,19},{19,3},{4,20},{20... | collective-permute-start | bytes 208904 | tf_op jit(solution)/shard_map/ppermute | solution.py:217
  25.0 9.8 %collective-permute-start.4 = (f32[136,128]{1,0:T(8,128)S(1)}, f32[136,128]{1,0:T(8,128)S(1)}, u32[]{:S(2)}, u32[]{:S(2)}) collective-permute-start(f32[136,128]{1,0:T(8,128)S(1)} %get-tuple-element.11.refs_0_), channel_id=1, source_target_pairs={{0,3},{1,2},{2,1},{3,0},{4,7},{5,6},{6,5},{7,4},{8,11},{9,10},{10,... | collective-permute-start | bytes 208904 | tf_op jit(solution)/shard_map/ppermute | solution.py:228
  25.6 9.2 %collective-permute-start.3 = (f32[136,128]{1,0:T(8,128)S(1)}, f32[136,128]{1,0:T(8,128)S(1)}, u32[]{:S(2)}, u32[]{:S(2)}) collective-permute-start(f32[136,128]{1,0:T(8,128)S(1)} %get-tuple-element.11.refs_0_), channel_id=1, source_target_pairs={{0,2},{1,3},{2,0},{3,1},{4,6},{5,7},{6,4},{7,5},{8,10},{9,11},{10,... | collective-permute-start | bytes 208904 | tf_op jit(solution)/shard_map/ppermute | solution.py:228
  26.6 8.2 %collective-permute-start.2 = (f32[136,128]{1,0:T(8,128)S(1)}, f32[136,128]{1,0:T(8,128)S(1)}, u32[]{:S(2)}, u32[]{:S(2)}) collective-permute-start(f32[136,128]{1,0:T(8,128)S(1)} %get-tuple-element.11.refs_0_), channel_id=1, source_target_pairs={{0,1},{1,0},{2,3},{3,2},{4,5},{5,4},{6,7},{7,6},{8,9},{9,8},{10,11... | collective-permute-start | bytes 208904 | tf_op jit(solution)/shard_map/ppermute | solution.py:228

commit v7 on v6

--- a/solution.py
+++ b/solution.py
@@ -78,6 +78,10 @@
     return terms.astype(jnp.bfloat16)
 
 
+def place_of(chip, chips):
+    return chip ^ (chips - 2)
+
+
 def pair_kernel(rows, mine_ref, came_ref, out_ref):
     chips, held, cols = out_ref.shape
     blocks = mine_ref.shape[0] - 2 * chips * rows
@@ -92,13 +96,13 @@
             check += jnp.dot(shares[1], second, preferred_element_type=jnp.float32)
             check = check[:blocks] + check[blocks : 2 * blocks] + check[2 * blocks : 3 * blocks]
             codes, power = encode(first.astype(jnp.float32) + second.astype(jnp.float32))
-            out_ref[chips - 1 - chip, pl.ds(half * (rows + blocks), rows), :] = codes.astype(jnp.int16)
+            out_ref[place_of(chip, chips), pl.ds(half * (rows + blocks), rows), :] = codes.astype(jnp.int16)
             powers.append(power)
             codes, power = encode(check)
-            out_ref[chips - 1 - chip, pl.ds(half * (rows + blocks) + rows, blocks), :] = codes.astype(jnp.int16)
+            out_ref[place_of(chip, chips), pl.ds(half * (rows + blocks) + rows, blocks), :] = codes.astype(jnp.int16)
             powers.append(power)
         powers.append(jnp.zeros((SUBLANES - 4, cols), jnp.int32))
-        out_ref[chips - 1 - chip, pl.ds(held - SUBLANES, SUBLANES), :] = jnp.concatenate(powers, axis=0).astype(
+        out_ref[place_of(chip, chips), pl.ds(held - SUBLANES, SUBLANES), :] = jnp.concatenate(powers, axis=0).astype(
             jnp.int16
         )
 
@@ -204,9 +208,9 @@
         mine,
         came,
     )
-    backward = [list(range(chips))[::-1]]
+    order = [[place_of(chip, chips) for chip in range(chips)]]
     received = lax.all_to_all(
-        coded, ("near", "side"), 0, 0, tiled=True, axis_index_groups=backward
+        coded, ("near", "side"), 0, 0, tiled=True, axis_index_groups=order
     )
     part = jax.ShapeDtypeStruct((rows, cols), jnp.float32)
     codes, mine, other = call(
@@ -273,6 +277,7 @@
             and blocks == SUBLANES
             and columns == far * near
             and replicas == side * core
+            and near & (near - 1) == 0
             and replicas & (replicas - 1) == 0
         )
         if tiled:

time: 36 us -> 35 us (0.972)
  blocking collectives: 22.7 us -> 21.8 us
    all_to_all x1, blocking collectives: 7.92 us -> 6.99 us  [small_body(): lax.all_to_all(square, ('near', 'side', 'core'), 0, 0, tiled=True, axis_i...]
where the time goes in v7:
time: 35 us; the launch traced here: 34.6 us
  blocking collectives  21.8 us (62%)
  starting transfers between devices  5.13 us (15%)
  Pallas kernels  3.86 us (11%)
  waiting for transfers between devices  3.19 us (9%)
  between operations  0.67 us (2%)
    all_to_all x1, blocking collectives, small_body(): lax.all_to_all(coded, ('near', 'side'), 0, 0, tiled=True, axis_index_grou...  14.8 us
    all_to_all x1, blocking collectives, small_body(): lax.all_to_all(square, ('near', 'side', 'core'), 0, 0, tiled=True, axis_i...  6.99 us
    ppermute x1, waiting for transfers between devices, small_body(): came = lax.ppermute(codes, 'far', [(0, 1), (1, 0)])  2.72 us
    ppermute x1, starting transfers between devices, small_body(): came = lax.ppermute(codes, 'far', [(0, 1), (1, 0)])  2.65 us
    pallas_call x2, Pallas kernels, pack(): pl.pallas_call(functools.partial(pack_kernel, mine), out_shape=jax.ShapeD...  2.15 us
    ppermute x3, starting transfers between devices, small_body(): totals.append(lax.ppermute(total, ('side', 'core'), swaps))  1.92 us
    pallas_call x4, Pallas kernels, call(): pl.pallas_call(kernel, out_shape=out_shape, in_specs=[vmem] * len(operand...  1.71 us
  transfers between devices with their start and end apart: 5, of which 2 were waited for; matrix products, arithmetic and copies ran while one was open for 0% of the time, Pallas kernels for 3%

profile of v7, /device:TPU:0, one launch (start us, length us, event | category | flops | bytes accessed | tf_op | source)
XLA Modules:
  0.0 34.6 jit_solution(6414843715547918806)
XLA Ops:
  0.6 1.1 %shard_map.42 = bf16[2056,128]{1,0:T(8,128)(2,1)S(1)} custom-call(bf16[128,4096]{1,0:T(8,128)(2,1)} %bitcast.8, s32[8,16]{1,0:T(8,128)} %bitcast.10), custom_call_target="tpu_custom_call" | custom-call | tf_op jit(solution)/shard_map/pallas_call | solution.py:180
  1.7 0.6 %collective-permute-start = (bf16[2056,128]{1,0:T(8,128)(2,1)S(1)}, bf16[2056,128]{1,0:T(8,128)(2,1)S(1)}, u32[]{:S(2)}, u32[]{:S(2)}) collective-permute-start(bf16[2056,128]{1,0:T(8,128)(2,1)S(1)} %shard_map.42), channel_id=1, source_target_pairs={{0,1},{1,0},{2,3},{3,2},{4,5},{5,4},{6,7},{7,6},{8,9},{9,8},{10,11... | collective-permute-start | bytes 1579016 | tf_op jit(solution)/shard_map/ppermute | solution.py:203
  2.3 1.1 %shard_map.41.mine_ref = bf16[2056,128]{1,0:T(8,128)(2,1)S(1)} custom-call(bf16[128,4096]{1,0:T(8,128)(2,1)} %bitcast.9, s32[8,16]{1,0:T(8,128)} %bitcast.11), custom_call_target="tpu_custom_call" | custom-call | tf_op jit(solution)/shard_map/pallas_call | solution.py:180
  3.4 0.5 %collective-permute-done.came_ref = bf16[2056,128]{1,0:T(8,128)(2,1)S(1)} collective-permute-done((bf16[2056,128]{1,0:T(8,128)(2,1)S(1)}, bf16[2056,128]{1,0:T(8,128)(2,1)S(1)}, u32[]{:S(2)}, u32[]{:S(2)}) %collective-permute-start) | collective-permute-done | bytes 526368 | tf_op jit(solution)/shard_map/ppermute | solution.py:203
  3.8 0.6 %shard_map.43 = s16[8,280,128]{2,1,0:T(8,128)(2,1)S(1)} custom-call(bf16[2056,128]{1,0:T(8,128)(2,1)S(1)} %shard_map.41.mine_ref, bf16[2056,128]{1,0:T(8,128)(2,1)S(1)} %collective-permute-done.came_ref), custom_call_target="tpu_custom_call" | custom-call | tf_op jit(solution)/shard_map/pallas_call | solution.py:194
  4.4 14.8 %all_to_all.16.recv_ref = s16[8,280,128]{2,1,0:T(8,128)(2,1)S(1)} all-to-all(s16[8,280,128]{2,1,0:T(8,128)(2,1)S(1)} %shard_map.43), channel_id=1, replica_groups={{12,14,8,10,4,6,0,2},{13,15,9,11,5,7,1,3},{28,30,24,26,20,22,16,18},{29..., dimensions={0} | all-to-all | bytes 1146880 | tf_op jit(solution)/shard_map/all_to_all | solution.py:212
  19.2 0.3 shard_map.44
  19.4 2.7 %collective-permute-start.1 = (s16[272,128]{1,0:T(8,128)(2,1)S(1)}, s16[272,128]{1,0:T(8,128)(2,1)S(1)}, u32[]{:S(2)}, u32[]{:S(2)}) collective-permute-start(s16[272,128]{1,0:T(8,128)(2,1)S(1)} %get-tuple-element.9), channel_id=1, source_target_pairs={{0,16},{16,0},{1,17},{17,1},{2,18},{18,2},{3,19},{19,3},{4,20},{20... | collective-permute-start | bytes 208904 | tf_op jit(solution)/shard_map/ppermute | solution.py:221
  22.1 2.7 %collective-permute-done.1.came_ref = s16[272,128]{1,0:T(8,128)(2,1)S(1)} collective-permute-done((s16[272,128]{1,0:T(8,128)(2,1)S(1)}, s16[272,128]{1,0:T(8,128)(2,1)S(1)}, u32[]{:S(2)}, u32[]{:S(2)}) %collective-permute-start.1) | collective-permute-done | bytes 69664 | tf_op jit(solution)/shard_map/ppermute | solution.py:221
  24.9 0.1 collective-permute-start.4
  24.9 1.1 %collective-permute-start.3 = (f32[136,128]{1,0:T(8,128)S(1)}, f32[136,128]{1,0:T(8,128)S(1)}, u32[]{:S(2)}, u32[]{:S(2)}) collective-permute-start(f32[136,128]{1,0:T(8,128)S(1)} %get-tuple-element.11.refs_0_), channel_id=1, source_target_pairs={{0,2},{1,3},{2,0},{3,1},{4,6},{5,7},{6,4},{7,5},{8,10},{9,11},{10,... | collective-permute-start | bytes 208904 | tf_op jit(solution)/shard_map/ppermute | solution.py:232
  26.0 0.8 %collective-permute-start.2 = (f32[136,128]{1,0:T(8,128)S(1)}, f32[136,128]{1,0:T(8,128)S(1)}, u32[]{:S(2)}, u32[]{:S(2)}) collective-permute-start(f32[136,128]{1,0:T(8,128)S(1)} %get-tuple-element.11.refs_0_), channel_id=1, source_target_pairs={{0,1},{1,0},{2,3},{3,2},{4,5},{5,4},{6,7},{7,6},{8,9},{9,8},{10,11... | collective-permute-start | bytes 208904 | tf_op jit(solution)/shard_map/ppermute | solution.py:232
  26.8 7.0 %all_to_all.17 = f32[16,1,128]{2,1,0:T(1,128)S(1)} all-to-all(f32[16,1,128]{2,1,0:T(1,128)S(1)} %bitcast.7), channel_id=1, replica_groups={{15,14,13,12,11,10,9,8,7,6,5,4,3,2,1,0},{31,30,29,28,27,26,25,24,23,22,..., dimensions={0} | all-to-all | bytes 16384 | tf_op jit(solution)/shard_map/all_to_all | solution.py:234
  33.8 0.0 collective-permute-done.4.refs_3_
  33.8 0.0 collective-permute-done.3.refs_2_
  33.8 0.0 collective-permute-done.2.refs_1_
  33.8 0.8 %shard_map.46 = (bf16[128,512]{1,0:T(8,128)(2,1)}, bf16[8,512]{1,0:T(8,128)(2,1)}) custom-call(f32[16,128]{1,0:T(8,128)S(1)} %bitcast.6, f32[136,128]{1,0:T(8,128)S(1)} %get-tuple-element.11.refs_0_, f32[136,128]{1,0:T(8,128)S(1)} %collective-permute-done.2.refs_1_, f32[136,128]{1,0:T(8,128)S(1)} %collective-permute-done.3.refs_2_, ...), custom_call_target="tpu_custom_call" | custom-call | tf_op jit(solution)/shard_map/pallas_call | solution.py:194
  (1 shorter events, 0.0 us)
Async XLA Ops:
  1.7 2.1 %collective-permute-start = (bf16[2056,128]{1,0:T(8,128)(2,1)S(1)}, bf16[2056,128]{1,0:T(8,128)(2,1)S(1)}, u32[]{:S(2)}, u32[]{:S(2)}) collective-permute-start(bf16[2056,128]{1,0:T(8,128)(2,1)S(1)} %shard_map.42), channel_id=1, source_target_pairs={{0,1},{1,0},{2,3},{3,2},{4,5},{5,4},{6,7},{7,6},{8,9},{9,8},{10,11... | collective-permute-start | bytes 1579016 | tf_op jit(solution)/shard_map/ppermute | solution.py:203
  19.4 5.4 %collective-permute-start.1 = (s16[272,128]{1,0:T(8,128)(2,1)S(1)}, s16[272,128]{1,0:T(8,128)(2,1)S(1)}, u32[]{:S(2)}, u32[]{:S(2)}) collective-permute-start(s16[272,128]{1,0:T(8,128)(2,1)S(1)} %get-tuple-element.9), channel_id=1, source_target_pairs={{0,16},{16,0},{1,17},{17,1},{2,18},{18,2},{3,19},{19,3},{4,20},{20... | collective-permute-start | bytes 208904 | tf_op jit(solution)/shard_map/ppermute | solution.py:221
  24.9 8.9 %collective-permute-start.4 = (f32[136,128]{1,0:T(8,128)S(1)}, f32[136,128]{1,0:T(8,128)S(1)}, u32[]{:S(2)}, u32[]{:S(2)}) collective-permute-start(f32[136,128]{1,0:T(8,128)S(1)} %get-tuple-element.11.refs_0_), channel_id=1, source_target_pairs={{0,3},{1,2},{2,1},{3,0},{4,7},{5,6},{6,5},{7,4},{8,11},{9,10},{10,... | collective-permute-start | bytes 208904 | tf_op jit(solution)/shard_map/ppermute | solution.py:232
  24.9 8.8 %collective-permute-start.3 = (f32[136,128]{1,0:T(8,128)S(1)}, f32[136,128]{1,0:T(8,128)S(1)}, u32[]{:S(2)}, u32[]{:S(2)}) collective-permute-start(f32[136,128]{1,0:T(8,128)S(1)} %get-tuple-element.11.refs_0_), channel_id=1, source_target_pairs={{0,2},{1,3},{2,0},{3,1},{4,6},{5,7},{6,4},{7,5},{8,10},{9,11},{10,... | collective-permute-start | bytes 208904 | tf_op jit(solution)/shard_map/ppermute | solution.py:232
  26.0 7.8 %collective-permute-start.2 = (f32[136,128]{1,0:T(8,128)S(1)}, f32[136,128]{1,0:T(8,128)S(1)}, u32[]{:S(2)}, u32[]{:S(2)}) collective-permute-start(f32[136,128]{1,0:T(8,128)S(1)} %get-tuple-element.11.refs_0_), channel_id=1, source_target_pairs={{0,1},{1,0},{2,3},{3,2},{4,5},{5,4},{6,7},{7,6},{8,9},{9,8},{10,11... | collective-permute-start | bytes 208904 | tf_op jit(solution)/shard_map/ppermute | solution.py:232

commit v8 on v7

--- a/solution.py
+++ b/solution.py
@@ -82,27 +82,40 @@
     return chip ^ (chips - 2)
 
 
-def pair_kernel(rows, mine_ref, came_ref, out_ref):
+def checks_of(shares, data):
+    blocks = shares.shape[0] // 4
+    check = jnp.dot(shares, data, preferred_element_type=jnp.float32)
+    return check[:blocks] + check[blocks : 2 * blocks] + check[2 * blocks : 3 * blocks]
+
+
+def check_kernel(rows, mine_ref, check_ref):
+    count = mine_ref.shape[0] // rows
+    blocks = mine_ref.shape[0] - count * rows
+    shares = shares_of(mine_ref[pl.ds(count * rows, blocks), :])
+    for i in range(count):
+        check_ref[pl.ds(i * blocks, blocks), :] = checks_of(shares, mine_ref[pl.ds(i * rows, rows), :])
+
+
+def pair_kernel(rows, mine_ref, check_ref, came_ref, out_ref):
     chips, held, cols = out_ref.shape
     blocks = mine_ref.shape[0] - 2 * chips * rows
-    weights = pl.ds(2 * chips * rows, blocks)
-    shares = shares_of(mine_ref[weights, :]), shares_of(came_ref[weights, :])
+    shares = shares_of(came_ref[pl.ds(2 * chips * rows, blocks), :])
     for chip in range(chips):
         powers = []
+        place = place_of(chip, chips)
         for half in range(2):
-            at = pl.ds((chip * 2 + half) * rows, rows)
+            i = chip * 2 + half
+            at = pl.ds(i * rows, rows)
             first, second = mine_ref[at, :], came_ref[at, :]
-            check = jnp.dot(shares[0], first, preferred_element_type=jnp.float32)
-            check += jnp.dot(shares[1], second, preferred_element_type=jnp.float32)
-            check = check[:blocks] + check[blocks : 2 * blocks] + check[2 * blocks : 3 * blocks]
+            check = check_ref[pl.ds(i * blocks, blocks), :] + checks_of(shares, second)
             codes, power = encode(first.astype(jnp.float32) + second.astype(jnp.float32))
-            out_ref[place_of(chip, chips), pl.ds(half * (rows + blocks), rows), :] = codes.astype(jnp.int16)
+            out_ref[place, pl.ds(half * (rows + blocks), rows), :] = codes.astype(jnp.int16)
             powers.append(power)
             codes, power = encode(check)
-            out_ref[place_of(chip, chips), pl.ds(half * (rows + blocks) + rows, blocks), :] = codes.astype(jnp.int16)
+            out_ref[place, pl.ds(half * (rows + blocks) + rows, blocks), :] = codes.astype(jnp.int16)
             powers.append(power)
         powers.append(jnp.zeros((SUBLANES - 4, cols), jnp.int32))
-        out_ref[place_of(chip, chips), pl.ds(held - SUBLANES, SUBLANES), :] = jnp.concatenate(powers, axis=0).astype(
+        out_ref[place, pl.ds(held - SUBLANES, SUBLANES), :] = jnp.concatenate(powers, axis=0).astype(
             jnp.int16
         )
 
@@ -202,10 +215,14 @@
     packed = pack(False)
     came = lax.ppermute(packed, "core", [(0, 1), (1, 0)])
     mine = pack(True)
+    checks = call(
+        functools.partial(check_kernel, rows), jax.ShapeDtypeStruct((far * chips * blocks, cols), jnp.float32), mine
+    )
     coded = call(
         functools.partial(pair_kernel, rows),
         jax.ShapeDtypeStruct((chips, far * (rows + blocks) + SUBLANES, cols), jnp.int16),
         mine,
+        checks,
         came,
     )
     order = [[place_of(chip, chips) for chip in range(chips)]]

time: 35 us -> 34.9 us (level)
    pallas_call x4 -> x5, Pallas kernels: 1.71 us -> 1.98 us  [call(): pl.pallas_call(kernel, out_shape=out_shape, in_specs=[vmem] * len(operand...]
  transfers between devices with their start and end apart: 5 -> 5, of which waited for: 2 -> 2; matrix products, arithmetic and copies ran while one was open for 0% -> 0% of each run, Pallas kernels for 3% -> 4%
where the time goes in v8:
time: 34.9 us; the launch traced here: 34.6 us
  blocking collectives  21.8 us (62%)
  starting transfers between devices  5.13 us (15%)
  Pallas kernels  4.13 us (12%)
  waiting for transfers between devices  2.87 us (8%)
  between operations  0.68 us (2%)
    all_to_all x1, blocking collectives, small_body(): lax.all_to_all(coded, ('near', 'side'), 0, 0, tiled=True, axis_index_grou...  14.8 us
    all_to_all x1, blocking collectives, small_body(): lax.all_to_all(square, ('near', 'side', 'core'), 0, 0, tiled=True, axis_i...  6.99 us
    ppermute x1, waiting for transfers between devices, small_body(): came = lax.ppermute(codes, 'far', [(0, 1), (1, 0)])  2.72 us
    ppermute x1, starting transfers between devices, small_body(): came = lax.ppermute(codes, 'far', [(0, 1), (1, 0)])  2.65 us
    pallas_call x2, Pallas kernels, pack(): pl.pallas_call(functools.partial(pack_kernel, mine), out_shape=jax.ShapeD...  2.15 us
    pallas_call x5, Pallas kernels, call(): pl.pallas_call(kernel, out_shape=out_shape, in_specs=[vmem] * len(operand...  1.98 us
    ppermute x3, starting transfers between devices, small_body(): totals.append(lax.ppermute(total, ('side', 'core'), swaps))  1.92 us
  transfers between devices with their start and end apart: 5, of which 2 were waited for; matrix products, arithmetic and copies ran while one was open for 0% of the time, Pallas kernels for 4%

profile of v8, /device:TPU:0, one launch (start us, length us, event | category | flops | bytes accessed | tf_op | source)
XLA Modules:
  0.0 34.6 jit_solution(2392081618741034854)
XLA Ops:
  0.6 1.1 %shard_map.43 = bf16[2056,128]{1,0:T(8,128)(2,1)S(1)} custom-call(bf16[128,4096]{1,0:T(8,128)(2,1)} %bitcast.8, s32[8,16]{1,0:T(8,128)} %bitcast.10), custom_call_target="tpu_custom_call" | custom-call | tf_op jit(solution)/shard_map/pallas_call | solution.py:193
  1.7 0.6 %collective-permute-start = (bf16[2056,128]{1,0:T(8,128)(2,1)S(1)}, bf16[2056,128]{1,0:T(8,128)(2,1)S(1)}, u32[]{:S(2)}, u32[]{:S(2)}) collective-permute-start(bf16[2056,128]{1,0:T(8,128)(2,1)S(1)} %shard_map.43), channel_id=1, source_target_pairs={{0,1},{1,0},{2,3},{3,2},{4,5},{5,4},{6,7},{7,6},{8,9},{9,8},{10,11... | collective-permute-start | bytes 1579016 | tf_op jit(solution)/shard_map/ppermute | solution.py:216
  2.3 1.1 %shard_map.41.mine_ref = bf16[2056,128]{1,0:T(8,128)(2,1)S(1)} custom-call(bf16[128,4096]{1,0:T(8,128)(2,1)} %bitcast.9, s32[8,16]{1,0:T(8,128)} %bitcast.11), custom_call_target="tpu_custom_call" | custom-call | tf_op jit(solution)/shard_map/pallas_call | solution.py:193
  3.4 0.3 shard_map.42.check_ref
  3.7 0.1 collective-permute-done.came_ref
  3.8 0.5 %shard_map.44 = s16[8,280,128]{2,1,0:T(8,128)(2,1)S(1)} custom-call(bf16[2056,128]{1,0:T(8,128)(2,1)S(1)} %shard_map.41.mine_ref, f32[128,128]{1,0:T(8,128)S(1)} %shard_map.42.check_ref, bf16[2056,128]{1,0:T(8,128)(2,1)S(1)} %collective-permute-done.came_ref), custom_call_target="tpu_custom_call" | custom-call | tf_op jit(solution)/shard_map/pallas_call | solution.py:207
  4.4 14.8 %all_to_all.16.recv_ref = s16[8,280,128]{2,1,0:T(8,128)(2,1)S(1)} all-to-all(s16[8,280,128]{2,1,0:T(8,128)(2,1)S(1)} %shard_map.44), channel_id=1, replica_groups={{12,14,8,10,4,6,0,2},{13,15,9,11,5,7,1,3},{28,30,24,26,20,22,16,18},{29..., dimensions={0} | all-to-all | bytes 1146880 | tf_op jit(solution)/shard_map/all_to_all | solution.py:229
  19.1 0.3 shard_map.45
  19.4 2.7 %collective-permute-start.1 = (s16[272,128]{1,0:T(8,128)(2,1)S(1)}, s16[272,128]{1,0:T(8,128)(2,1)S(1)}, u32[]{:S(2)}, u32[]{:S(2)}) collective-permute-start(s16[272,128]{1,0:T(8,128)(2,1)S(1)} %get-tuple-element.9), channel_id=1, source_target_pairs={{0,16},{16,0},{1,17},{17,1},{2,18},{18,2},{3,19},{19,3},{4,20},{20... | collective-permute-start | bytes 208904 | tf_op jit(solution)/shard_map/ppermute | solution.py:238
  22.1 2.7 %collective-permute-done.1.came_ref = s16[272,128]{1,0:T(8,128)(2,1)S(1)} collective-permute-done((s16[272,128]{1,0:T(8,128)(2,1)S(1)}, s16[272,128]{1,0:T(8,128)(2,1)S(1)}, u32[]{:S(2)}, u32[]{:S(2)}) %collective-permute-start.1) | collective-permute-done | bytes 69664 | tf_op jit(solution)/shard_map/ppermute | solution.py:238
  24.8 0.1 collective-permute-start.4
  24.9 1.1 %collective-permute-start.3 = (f32[136,128]{1,0:T(8,128)S(1)}, f32[136,128]{1,0:T(8,128)S(1)}, u32[]{:S(2)}, u32[]{:S(2)}) collective-permute-start(f32[136,128]{1,0:T(8,128)S(1)} %get-tuple-element.11.refs_0_), channel_id=1, source_target_pairs={{0,2},{1,3},{2,0},{3,1},{4,6},{5,7},{6,4},{7,5},{8,10},{9,11},{10,... | collective-permute-start | bytes 208904 | tf_op jit(solution)/shard_map/ppermute | solution.py:249
  26.0 0.8 %collective-permute-start.2 = (f32[136,128]{1,0:T(8,128)S(1)}, f32[136,128]{1,0:T(8,128)S(1)}, u32[]{:S(2)}, u32[]{:S(2)}) collective-permute-start(f32[136,128]{1,0:T(8,128)S(1)} %get-tuple-element.11.refs_0_), channel_id=1, source_target_pairs={{0,1},{1,0},{2,3},{3,2},{4,5},{5,4},{6,7},{7,6},{8,9},{9,8},{10,11... | collective-permute-start | bytes 208904 | tf_op jit(solution)/shard_map/ppermute | solution.py:249
  26.8 7.0 %all_to_all.17 = f32[16,1,128]{2,1,0:T(1,128)S(1)} all-to-all(f32[16,1,128]{2,1,0:T(1,128)S(1)} %bitcast.7), channel_id=1, replica_groups={{15,14,13,12,11,10,9,8,7,6,5,4,3,2,1,0},{31,30,29,28,27,26,25,24,23,22,..., dimensions={0} | all-to-all | bytes 16384 | tf_op jit(solution)/shard_map/all_to_all | solution.py:251
  33.7 0.0 collective-permute-done.4.refs_3_
  33.7 0.0 collective-permute-done.3.refs_2_
  33.7 0.0 collective-permute-done.2.refs_1_
  33.8 0.8 %shard_map.47 = (bf16[128,512]{1,0:T(8,128)(2,1)}, bf16[8,512]{1,0:T(8,128)(2,1)}) custom-call(f32[16,128]{1,0:T(8,128)S(1)} %bitcast.6, f32[136,128]{1,0:T(8,128)S(1)} %get-tuple-element.11.refs_0_, f32[136,128]{1,0:T(8,128)S(1)} %collective-permute-done.2.refs_1_, f32[136,128]{1,0:T(8,128)S(1)} %collective-permute-done.3.refs_2_, ...), custom_call_target="tpu_custom_call" | custom-call | tf_op jit(solution)/shard_map/pallas_call | solution.py:207
  (1 shorter events, 0.0 us)
Async XLA Ops:
  1.7 2.1 %collective-permute-start = (bf16[2056,128]{1,0:T(8,128)(2,1)S(1)}, bf16[2056,128]{1,0:T(8,128)(2,1)S(1)}, u32[]{:S(2)}, u32[]{:S(2)}) collective-permute-start(bf16[2056,128]{1,0:T(8,128)(2,1)S(1)} %shard_map.43), channel_id=1, source_target_pairs={{0,1},{1,0},{2,3},{3,2},{4,5},{5,4},{6,7},{7,6},{8,9},{9,8},{10,11... | collective-permute-start | bytes 1579016 | tf_op jit(solution)/shard_map/ppermute | solution.py:216
  19.4 5.4 %collective-permute-start.1 = (s16[272,128]{1,0:T(8,128)(2,1)S(1)}, s16[272,128]{1,0:T(8,128)(2,1)S(1)}, u32[]{:S(2)}, u32[]{:S(2)}) collective-permute-start(s16[272,128]{1,0:T(8,128)(2,1)S(1)} %get-tuple-element.9), channel_id=1, source_target_pairs={{0,16},{16,0},{1,17},{17,1},{2,18},{18,2},{3,19},{19,3},{4,20},{20... | collective-permute-start | bytes 208904 | tf_op jit(solution)/shard_map/ppermute | solution.py:238
  24.8 8.9 %collective-permute-start.4 = (f32[136,128]{1,0:T(8,128)S(1)}, f32[136,128]{1,0:T(8,128)S(1)}, u32[]{:S(2)}, u32[]{:S(2)}) collective-permute-start(f32[136,128]{1,0:T(8,128)S(1)} %get-tuple-element.11.refs_0_), channel_id=1, source_target_pairs={{0,3},{1,2},{2,1},{3,0},{4,7},{5,6},{6,5},{7,4},{8,11},{9,10},{10,... | collective-permute-start | bytes 208904 | tf_op jit(solution)/shard_map/ppermute | solution.py:249
  24.9 8.8 %collective-permute-start.3 = (f32[136,128]{1,0:T(8,128)S(1)}, f32[136,128]{1,0:T(8,128)S(1)}, u32[]{:S(2)}, u32[]{:S(2)}) collective-permute-start(f32[136,128]{1,0:T(8,128)S(1)} %get-tuple-element.11.refs_0_), channel_id=1, source_target_pairs={{0,2},{1,3},{2,0},{3,1},{4,6},{5,7},{6,4},{7,5},{8,10},{9,11},{10,... | collective-permute-start | bytes 208904 | tf_op jit(solution)/shard_map/ppermute | solution.py:249
  26.0 7.8 %collective-permute-start.2 = (f32[136,128]{1,0:T(8,128)S(1)}, f32[136,128]{1,0:T(8,128)S(1)}, u32[]{:S(2)}, u32[]{:S(2)}) collective-permute-start(f32[136,128]{1,0:T(8,128)S(1)} %get-tuple-element.11.refs_0_), channel_id=1, source_target_pairs={{0,1},{1,0},{2,3},{3,2},{4,5},{5,4},{6,7},{7,6},{8,9},{9,8},{10,11... | collective-permute-start | bytes 208904 | tf_op jit(solution)/shard_map/ppermute | solution.py:249

commit v9 on v8

--- a/solution.py
+++ b/solution.py
@@ -12,6 +12,7 @@
 SUBLANES = 8
 FULL = 32767.0
 LEAST, MOST = -126, 126
+STEPS = 128
 GRANT = pltpu.CompilerParams(vmem_limit_bytes=8 * 1024 * 1024)
 
 
@@ -57,14 +58,14 @@
 
 def encode(values):
     top = jnp.maximum(jnp.max(jnp.abs(values), axis=0, keepdims=True), 2.0**LEAST)
-    power = jnp.clip(jnp.ceil(jnp.log2(top)), float(LEAST), float(MOST))
-    codes = jnp.round(values * jnp.exp2(-power) * FULL)
+    power = jnp.clip(jnp.ceil(jnp.log2(top) * STEPS), float(LEAST * STEPS), float(MOST * STEPS))
+    codes = jnp.round(values * jnp.exp2(power * (-1.0 / STEPS)) * FULL)
     return jnp.clip(codes, -FULL, FULL).astype(jnp.int32), power.astype(jnp.int32)
 
 
 def decode(codes, power):
     values = codes.astype(jnp.int32).astype(jnp.float32) * (1.0 / FULL)
-    return values * jnp.exp2(power.astype(jnp.float32))
+    return values * jnp.exp2(power.astype(jnp.float32) * (1.0 / STEPS))
 
 
 def shares_of(weights):

time: 34.9 us -> 34.9 us (level)
  no operation moved by 1% of the time
where the time goes in v9:
time: 34.9 us; the launch traced here: 34.6 us
  blocking collectives  21.8 us (62%)
  starting transfers between devices  5.13 us (15%)
  Pallas kernels  4.13 us (12%)
  waiting for transfers between devices  2.87 us (8%)
  between operations  0.68 us (2%)
    all_to_all x1, blocking collectives, small_body(): lax.all_to_all(coded, ('near', 'side'), 0, 0, tiled=True, axis_index_grou...  14.8 us
    all_to_all x1, blocking collectives, small_body(): lax.all_to_all(square, ('near', 'side', 'core'), 0, 0, tiled=True, axis_i...  6.99 us
    ppermute x1, waiting for transfers between devices, small_body(): came = lax.ppermute(codes, 'far', [(0, 1), (1, 0)])  2.72 us
    ppermute x1, starting transfers between devices, small_body(): came = lax.ppermute(codes, 'far', [(0, 1), (1, 0)])  2.65 us
    pallas_call x2, Pallas kernels, pack(): pl.pallas_call(functools.partial(pack_kernel, mine), out_shape=jax.ShapeD...  2.15 us
    pallas_call x5, Pallas kernels, call(): pl.pallas_call(kernel, out_shape=out_shape, in_specs=[vmem] * len(operand...  1.98 us
    ppermute x3, starting transfers between devices, small_body(): totals.append(lax.ppermute(total, ('side', 'core'), swaps))  1.92 us
  transfers between devices with their start and end apart: 5, of which 2 were waited for; matrix products, arithmetic and copies ran while one was open for 0% of the time, Pallas kernels for 4%

profile of v9, /device:TPU:0, one launch (start us, length us, event | category | flops | bytes accessed | tf_op | source)
XLA Modules:
  0.0 34.6 jit_solution(4444181988872469655)
XLA Ops:
  0.6 1.1 %shard_map.43 = bf16[2056,128]{1,0:T(8,128)(2,1)S(1)} custom-call(bf16[128,4096]{1,0:T(8,128)(2,1)} %bitcast.8, s32[8,16]{1,0:T(8,128)} %bitcast.10), custom_call_target="tpu_custom_call" | custom-call | tf_op jit(solution)/shard_map/pallas_call | solution.py:194
  1.7 0.6 %collective-permute-start = (bf16[2056,128]{1,0:T(8,128)(2,1)S(1)}, bf16[2056,128]{1,0:T(8,128)(2,1)S(1)}, u32[]{:S(2)}, u32[]{:S(2)}) collective-permute-start(bf16[2056,128]{1,0:T(8,128)(2,1)S(1)} %shard_map.43), channel_id=1, source_target_pairs={{0,1},{1,0},{2,3},{3,2},{4,5},{5,4},{6,7},{7,6},{8,9},{9,8},{10,11... | collective-permute-start | bytes 1579016 | tf_op jit(solution)/shard_map/ppermute | solution.py:217
  2.3 1.1 %shard_map.41.mine_ref = bf16[2056,128]{1,0:T(8,128)(2,1)S(1)} custom-call(bf16[128,4096]{1,0:T(8,128)(2,1)} %bitcast.9, s32[8,16]{1,0:T(8,128)} %bitcast.11), custom_call_target="tpu_custom_call" | custom-call | tf_op jit(solution)/shard_map/pallas_call | solution.py:194
  3.4 0.3 shard_map.42.check_ref
  3.7 0.1 collective-permute-done.came_ref
  3.8 0.5 %shard_map.44 = s16[8,280,128]{2,1,0:T(8,128)(2,1)S(1)} custom-call(bf16[2056,128]{1,0:T(8,128)(2,1)S(1)} %shard_map.41.mine_ref, f32[128,128]{1,0:T(8,128)S(1)} %shard_map.42.check_ref, bf16[2056,128]{1,0:T(8,128)(2,1)S(1)} %collective-permute-done.came_ref), custom_call_target="tpu_custom_call" | custom-call | tf_op jit(solution)/shard_map/pallas_call | solution.py:208
  4.4 14.8 %all_to_all.16.recv_ref = s16[8,280,128]{2,1,0:T(8,128)(2,1)S(1)} all-to-all(s16[8,280,128]{2,1,0:T(8,128)(2,1)S(1)} %shard_map.44), channel_id=1, replica_groups={{12,14,8,10,4,6,0,2},{13,15,9,11,5,7,1,3},{28,30,24,26,20,22,16,18},{29..., dimensions={0} | all-to-all | bytes 1146880 | tf_op jit(solution)/shard_map/all_to_all | solution.py:230
  19.1 0.3 shard_map.45
  19.4 2.7 %collective-permute-start.1 = (s16[272,128]{1,0:T(8,128)(2,1)S(1)}, s16[272,128]{1,0:T(8,128)(2,1)S(1)}, u32[]{:S(2)}, u32[]{:S(2)}) collective-permute-start(s16[272,128]{1,0:T(8,128)(2,1)S(1)} %get-tuple-element.9), channel_id=1, source_target_pairs={{0,16},{16,0},{1,17},{17,1},{2,18},{18,2},{3,19},{19,3},{4,20},{20... | collective-permute-start | bytes 208904 | tf_op jit(solution)/shard_map/ppermute | solution.py:239
  22.1 2.7 %collective-permute-done.1.came_ref = s16[272,128]{1,0:T(8,128)(2,1)S(1)} collective-permute-done((s16[272,128]{1,0:T(8,128)(2,1)S(1)}, s16[272,128]{1,0:T(8,128)(2,1)S(1)}, u32[]{:S(2)}, u32[]{:S(2)}) %collective-permute-start.1) | collective-permute-done | bytes 69664 | tf_op jit(solution)/shard_map/ppermute | solution.py:239
  24.8 0.1 collective-permute-start.4
  24.9 1.1 %collective-permute-start.3 = (f32[136,128]{1,0:T(8,128)S(1)}, f32[136,128]{1,0:T(8,128)S(1)}, u32[]{:S(2)}, u32[]{:S(2)}) collective-permute-start(f32[136,128]{1,0:T(8,128)S(1)} %get-tuple-element.11.refs_0_), channel_id=1, source_target_pairs={{0,2},{1,3},{2,0},{3,1},{4,6},{5,7},{6,4},{7,5},{8,10},{9,11},{10,... | collective-permute-start | bytes 208904 | tf_op jit(solution)/shard_map/ppermute | solution.py:250
  26.0 0.8 %collective-permute-start.2 = (f32[136,128]{1,0:T(8,128)S(1)}, f32[136,128]{1,0:T(8,128)S(1)}, u32[]{:S(2)}, u32[]{:S(2)}) collective-permute-start(f32[136,128]{1,0:T(8,128)S(1)} %get-tuple-element.11.refs_0_), channel_id=1, source_target_pairs={{0,1},{1,0},{2,3},{3,2},{4,5},{5,4},{6,7},{7,6},{8,9},{9,8},{10,11... | collective-permute-start | bytes 208904 | tf_op jit(solution)/shard_map/ppermute | solution.py:250
  26.8 7.0 %all_to_all.17 = f32[16,1,128]{2,1,0:T(1,128)S(1)} all-to-all(f32[16,1,128]{2,1,0:T(1,128)S(1)} %bitcast.7), channel_id=1, replica_groups={{15,14,13,12,11,10,9,8,7,6,5,4,3,2,1,0},{31,30,29,28,27,26,25,24,23,22,..., dimensions={0} | all-to-all | bytes 16384 | tf_op jit(solution)/shard_map/all_to_all | solution.py:252
  33.7 0.0 collective-permute-done.4.refs_3_
  33.7 0.0 collective-permute-done.3.refs_2_
  33.7 0.0 collective-permute-done.2.refs_1_
  33.8 0.8 %shard_map.47 = (bf16[128,512]{1,0:T(8,128)(2,1)}, bf16[8,512]{1,0:T(8,128)(2,1)}) custom-call(f32[16,128]{1,0:T(8,128)S(1)} %bitcast.6, f32[136,128]{1,0:T(8,128)S(1)} %get-tuple-element.11.refs_0_, f32[136,128]{1,0:T(8,128)S(1)} %collective-permute-done.2.refs_1_, f32[136,128]{1,0:T(8,128)S(1)} %collective-permute-done.3.refs_2_, ...), custom_call_target="tpu_custom_call" | custom-call | tf_op jit(solution)/shard_map/pallas_call | solution.py:208
  (1 shorter events, 0.0 us)
Async XLA Ops:
  1.7 2.1 %collective-permute-start = (bf16[2056,128]{1,0:T(8,128)(2,1)S(1)}, bf16[2056,128]{1,0:T(8,128)(2,1)S(1)}, u32[]{:S(2)}, u32[]{:S(2)}) collective-permute-start(bf16[2056,128]{1,0:T(8,128)(2,1)S(1)} %shard_map.43), channel_id=1, source_target_pairs={{0,1},{1,0},{2,3},{3,2},{4,5},{5,4},{6,7},{7,6},{8,9},{9,8},{10,11... | collective-permute-start | bytes 1579016 | tf_op jit(solution)/shard_map/ppermute | solution.py:217
  19.4 5.4 %collective-permute-start.1 = (s16[272,128]{1,0:T(8,128)(2,1)S(1)}, s16[272,128]{1,0:T(8,128)(2,1)S(1)}, u32[]{:S(2)}, u32[]{:S(2)}) collective-permute-start(s16[272,128]{1,0:T(8,128)(2,1)S(1)} %get-tuple-element.9), channel_id=1, source_target_pairs={{0,16},{16,0},{1,17},{17,1},{2,18},{18,2},{3,19},{19,3},{4,20},{20... | collective-permute-start | bytes 208904 | tf_op jit(solution)/shard_map/ppermute | solution.py:239
  24.8 8.9 %collective-permute-start.4 = (f32[136,128]{1,0:T(8,128)S(1)}, f32[136,128]{1,0:T(8,128)S(1)}, u32[]{:S(2)}, u32[]{:S(2)}) collective-permute-start(f32[136,128]{1,0:T(8,128)S(1)} %get-tuple-element.11.refs_0_), channel_id=1, source_target_pairs={{0,3},{1,2},{2,1},{3,0},{4,7},{5,6},{6,5},{7,4},{8,11},{9,10},{10,... | collective-permute-start | bytes 208904 | tf_op jit(solution)/shard_map/ppermute | solution.py:250
  24.9 8.8 %collective-permute-start.3 = (f32[136,128]{1,0:T(8,128)S(1)}, f32[136,128]{1,0:T(8,128)S(1)}, u32[]{:S(2)}, u32[]{:S(2)}) collective-permute-start(f32[136,128]{1,0:T(8,128)S(1)} %get-tuple-element.11.refs_0_), channel_id=1, source_target_pairs={{0,2},{1,3},{2,0},{3,1},{4,6},{5,7},{6,4},{7,5},{8,10},{9,11},{10,... | collective-permute-start | bytes 208904 | tf_op jit(solution)/shard_map/ppermute | solution.py:250
  26.0 7.8 %collective-permute-start.2 = (f32[136,128]{1,0:T(8,128)S(1)}, f32[136,128]{1,0:T(8,128)S(1)}, u32[]{:S(2)}, u32[]{:S(2)}) collective-permute-start(f32[136,128]{1,0:T(8,128)S(1)} %get-tuple-element.11.refs_0_), channel_id=1, source_target_pairs={{0,1},{1,0},{2,3},{3,2},{4,5},{5,4},{6,7},{7,6},{8,9},{9,8},{10,11... | collective-permute-start | bytes 208904 | tf_op jit(solution)/shard_map/ppermute | solution.py:250
